TPU v7x, 256 devices: a whole 4x4x8 slice. The times are simulated.
256 devices in a mesh: seq: 64 (over y, z, core), tensor: 4 (over x).
Axes of the slice: x: 4, y: 4, z: 8, core: 2. Of those that a mesh axis runs over, the one named last changes fastest.
Arguments:
- hidden_in: bfloat16 [8192, 8192], P('seq', 'tensor'), may hold values from -6 to 6
- grad_out: bfloat16 [8192, 8192], P('seq', 'tensor'), may hold values from -6 to 6
- slot_tokens: int32 [1024], P('seq'), may hold values from 0 to 127, as said below
- live_counts: int32 [64], P('seq'), may hold values from 5 to 16, as said below
- norm_gain: float32 [8192], P('tensor'), may hold values from 0.5 to 1.5
- router_weight: float32 [8192], P('tensor'), may hold values from -0.0625 to 0.0625
- gate_weight: bfloat16 [8192, 24576], P('tensor', 'seq'), may hold values from -0.0625 to 0.0625
- up_weight: bfloat16 [8192, 24576], P('tensor', 'seq'), may hold values from -0.0625 to 0.0625
- down_weight: bfloat16 [24576, 8192], P('seq', 'tensor'), may hold values from -0.0390625 to 0.0390625
Outputs:
- grad_in: bfloat16 [8192, 8192], P('seq', 'tensor')
- grad_gate: bfloat16 [8192, 24576], P('tensor', 'seq')
- grad_up: bfloat16 [8192, 24576], P('tensor', 'seq')
- grad_down: bfloat16 [24576, 8192], P('seq', 'tensor')
- grad_gain: float32 [8192], P('tensor')
- grad_router: float32 [8192], P('tensor')
Inputs may be any that keep to these rules, and one draw needn't show every extreme that they name: `slot_tokens`: slot p belongs to index p // 16 of seq; the live slots of one index hold distinct positions, the others hold arbitrary positions of that index. `live_counts`: in every draw some index of seq has all 16 slots live.
All inputs are finite; a program needn't handle non-finite values.
Results may differ from a plain program's by a relative error of at most 0.0077.
Values may be sent and summed in bfloat16 or wider, within the bound.
A program may use at most 128 MiB of HBM per device.

v0:
```python
import math

import jax
import jax.numpy as jnp
from jax import lax
from jax.sharding import PartitionSpec as P

norm_eps = 1e-06


def from_everyone(array, axis):
    count = lax.axis_size(axis)
    return lax.all_to_all(
        jnp.broadcast_to(array[None], (count, *array.shape)), axis, 0, 0, tiled=True
    )


def of_everyone(array, axis):
    return from_everyone(array, axis).sum(axis=0)


def sent_together(arrays, axis, dim, along):
    widths = [a.shape[along] for a in arrays]
    both = jnp.concatenate(arrays, axis=along)
    filled = lax.all_gather(both, axis, axis=dim, tiled=True)
    return tuple(jnp.split(filled, [sum(widths[:k]) for k in range(1, len(widths))], axis=along))


def in_one_piece(arrays, axis, dim, along):
    widths = [math.prod(a.shape[along:]) for a in arrays]
    both = jnp.concatenate(
        [a.reshape(*a.shape[:along], w) for a, w in zip(arrays, widths)], axis=along
    )
    filled = lax.psum_scatter(both, axis, scatter_dimension=dim, tiled=True)
    parts = jnp.split(filled, [sum(widths[:k]) for k in range(1, len(widths))], axis=along)
    return tuple(
        (b.reshape(*filled.shape[:along], *a.shape[along:]) for a, b in zip(arrays, parts))
    )


def split_up(array, dim, count):
    dims = array.shape
    parts = array.reshape(*dims[:dim], count, dims[dim] // count, *dims[dim + 1 :])
    return jnp.moveaxis(parts, dim, 0)


def summed_on_arrival(array, axis, dim):
    count = lax.axis_size(axis)
    parts = lax.all_to_all(split_up(array, dim, count), axis, 0, 0, tiled=True)
    return jnp.sum(parts.astype(jnp.float32), axis=0)


def in_one(arrays, axis):
    ends = [0]
    for a in arrays:
        ends.append(ends[-1] + a.size)
    subtotal = of_everyone(jnp.concatenate([a.ravel() for a in arrays]), axis)
    return tuple((subtotal[b:e].reshape(a.shape) for a, b, e in zip(arrays, ends, ends[1:])))


def silu_parts(gate):
    sig = jax.nn.sigmoid(gate)
    return (gate * sig, sig * (1.0 + gate * (1.0 - sig)))


def gate_backward(gate, upper, back, logits):
    act, slope = silu_parts(gate)
    hidden = act * upper
    weighted = (hidden * logits[:, None]).astype(jnp.bfloat16)
    router_grad = jnp.sum(hidden * back, axis=1)
    d_hidden = logits[:, None] * back
    d_gate = (d_hidden * upper * slope).astype(jnp.bfloat16)
    d_up = (d_hidden * act).astype(jnp.bfloat16)
    return (weighted, d_gate, d_up, router_grad)


def body(
    hidden_in,
    grad_out,
    slot_tokens,
    live_counts,
    norm_gain,
    router_weight,
    gate_weight,
    up_weight,
    down_weight,
):
    slot_count = slot_tokens.shape[0]
    width_total = hidden_in.shape[1] * lax.axis_size("tensor")
    live_rows = lax.iota(jnp.int32, slot_count) < live_counts[0]
    picked = jnp.take(hidden_in, slot_tokens, axis=0)
    upstream = jnp.where(
        live_rows[:, None], jnp.take(grad_out, slot_tokens, axis=0), jnp.zeros((), jnp.bfloat16)
    )
    wide = picked.astype(jnp.float32)
    squares = of_everyone(jnp.sum(wide * wide, axis=1), "tensor")
    inverse = lax.rsqrt(squares / width_total + norm_eps)[:, None]
    scaled = wide * inverse
    normed = (scaled * norm_gain).astype(jnp.bfloat16)
    all_normed, all_upstream = sent_together((normed, upstream), "seq", 0, 1)
    gate_part = jnp.dot(all_normed, gate_weight, preferred_element_type=jnp.float32)
    upper_part = jnp.dot(all_normed, up_weight, preferred_element_type=jnp.float32)
    back_part = jnp.einsum(
        "pd,fd->pf", all_upstream, down_weight, preferred_element_type=jnp.float32
    )
    logit_part = jnp.dot(
        all_normed, router_weight.astype(jnp.bfloat16), preferred_element_type=jnp.float32
    )
    gate, upper, back, logits = in_one_piece(
        (gate_part, upper_part, back_part, logit_part), "tensor", 0, 1
    )
    weighted, d_gate, d_up, router_grad = gate_backward(gate, upper, back, logits)
    weighted, d_gate, d_up = (
        lax.all_gather(weighted, "tensor", axis=0, tiled=True),
        lax.all_gather(d_gate, "tensor", axis=0, tiled=True),
        lax.all_gather(d_up, "tensor", axis=0, tiled=True),
    )
    router_grad = lax.all_gather(router_grad, "tensor", axis=0, tiled=True)
    grad_gate = jnp.einsum("pd,pf->df", all_normed, d_gate, preferred_element_type=jnp.float32)
    grad_up = jnp.einsum("pd,pf->df", all_normed, d_up, preferred_element_type=jnp.float32)
    grad_down = jnp.einsum("pf,pd->fd", weighted, all_upstream, preferred_element_type=jnp.float32)
    router_part = jnp.dot(
        router_grad, all_normed.astype(jnp.float32), precision=lax.Precision.HIGHEST
    )
    total = jnp.einsum("pf,df->pd", d_gate, gate_weight, preferred_element_type=jnp.float32)
    total = total + jnp.einsum("pf,df->pd", d_up, up_weight, preferred_element_type=jnp.float32)
    d_normed = summed_on_arrival(
        (total + router_grad[:, None] * router_weight).astype(jnp.bfloat16), "seq", 0
    )
    d_scaled = d_normed * norm_gain
    inner = lax.psum(jnp.sum(d_scaled * scaled, axis=1), "tensor") / width_total
    d_picked = inverse * (d_scaled - scaled * inner[:, None])
    d_picked = jnp.where(live_rows[:, None], d_picked, jnp.zeros((), jnp.float32))
    gain_part = jnp.sum(d_normed * scaled, axis=0)
    gain_total, router_total, count_total = in_one(
        (gain_part, router_part, live_counts[0].astype(jnp.float32)), "seq"
    )
    count_scale = lax.rsqrt(count_total)
    grad_in = grad_out.astype(jnp.float32).at[slot_tokens].add(d_picked).astype(jnp.bfloat16)
    gate_out = (count_scale * grad_gate).astype(jnp.bfloat16)
    up_out = (count_scale * grad_up).astype(jnp.bfloat16)
    down_out = (count_scale * grad_down).astype(jnp.bfloat16)
    return (
        grad_in,
        gate_out,
        up_out,
        down_out,
        count_scale * gain_total,
        count_scale * router_total,
    )


def solution(mesh):
    in_specs = (
        P("seq", "tensor"),
        P("seq", "tensor"),
        P("seq"),
        P("seq"),
        P("tensor"),
        P("tensor"),
        P("tensor", "seq"),
        P("tensor", "seq"),
        P("seq", "tensor"),
    )
    out_specs = (
        P("seq", "tensor"),
        P("tensor", "seq"),
        P("tensor", "seq"),
        P("seq", "tensor"),
        P("tensor"),
        P("tensor"),
    )
    return jax.shard_map(body, mesh=mesh, in_specs=in_specs, out_specs=out_specs, check_vma=False)
```

profile of v0, /device:TPU:2, one launch (start us, length us, event | category | flops | bytes accessed | tf_op | source)
XLA Modules:
  0.0 389.5 jit_solution(16129779356121668516)
XLA Ops:
  9.3 1.8 gather_fusion
  11.8 5.4 %all-to-all-start = ((f32[4,1,16]{2,1,0:T(1,128)}), f32[4,1,16]{2,1,0:T(1,128)S(1)}, u32[]{:S(2)}, u32[]{:S(2)}) async-start(f32[4,1,16]{2,1,0:T(1,128)} %broadcast_in_dim.56), calls=%async_computation | async-start | bytes 4096 | tf_op jit(solution)/shard_map/all_to_all | solution.py:13
  17.3 1.8 gather_fusion.1
  19.1 1.9 all-to-all-done
  21.1 0.8 fusion.24
  23.3 83.8 %all-gather.3.cloned.1.call-done = bf16[1024,4096]{1,0:T(8,128)(2,1)} async-done(((bf16[16,4096]{1,0:T(8,128)(2,1)}), bf16[1024,4096]{1,0:T(8,128)(2,1)}) %all-gather.3.cloned.1.call-update) | async-done | bytes 8388624 | tf_op jit(solution)/shard_map/all_gather | solution.py:25
  107.1 4.6 %fusion.12 = f32[1024,384]{0,1:T(8,128)S(1)} fusion(bf16[2048,384]{1,0:T(8,128)(2,1)} %param.18, bf16[1024,4096]{1,0:T(8,128)(2,1)} %all-gather.3.cloned.1.call-done), kind=kOutput, calls=%fused_computation.19 | convolution fusion | flops 1610612736 | bytes 7340032 | tf_op jit(solution)/shard_map/dot_general | solution.py:102
  112.2 1.8 fusion.14
  114.1 1.8 fusion.2
  115.9 1.2 fusion.16
  117.1 2.6 pad_maximum_fusion
  119.7 49.6 %reduce-scatter.2.cloned.1.call-done = f32[256,1153]{0,1:T(8,128)} async-done(((f32[1024,1153]{0,1:T(8,128)}), f32[256,1153]{0,1:T(8,128)}) %reduce-scatter.2.cloned.1.call-update) | async-done | bytes 1180688 | tf_op jit(solution)/shard_map/reduce_scatter | solution.py:34
  170.0 2.2 multiply_convert_fusion.3
  172.2 12.7 %all_gather.16 = bf16[1024,384]{0,1:T(8,128)(2,1)S(1)} all-gather(bf16[256,384]{0,1:T(8,128)(2,1)S(1)} %get-tuple-element.11), channel_id=1, replica_groups=mesh['seq'=64,'tensor'=4] {'tensor'}, dimensions={0}, use_global_device_ids=true | all-gather | bytes 983040 | tf_op jit(solution)/shard_map/all_gather | solution.py:115
  184.9 2.4 fusion.39
  187.3 13.8 %all_gather.17 = bf16[1024,384]{0,1:T(8,128)(2,1)S(1)} all-gather(bf16[256,384]{0,1:T(8,128)(2,1)S(1)} %get-tuple-element.10), channel_id=1, replica_groups=mesh['seq'=64,'tensor'=4] {'tensor'}, dimensions={0}, use_global_device_ids=true | all-gather | bytes 983040 | tf_op jit(solution)/shard_map/all_gather | solution.py:116
  201.1 10.7 %all-gather = f32[4,1,256]{2,1,0:T(1,128)S(1)} all-gather(f32[1,1,256]{2,1,0:T(1,128)S(1)} %bitcast.35), channel_id=1, replica_groups=mesh['seq'=64,'tensor'=4] {'tensor'}, dimensions={0}, use_global_device_ids=true | all-gather | bytes 5120 | tf_op jit(solution)/shard_map/all_gather | solution.py:118
  211.7 5.3 %add_convert_fusion = bf16[1024,2048]{1,0:T(8,128)(2,1)} fusion(f32[1024,2048]{1,0:T(8,128)S(1)} %fusion.39, bf16[1024,384]{0,1:T(8,128)(2,1)S(1)} %all_gather.17, bf16[2048,384]{1,0:T(8,128)(2,1)S(1)} %copy-done.8, f32[2048]{0:T(1024)S(1)} %copy-done.6, f32[1024]{0:T(1024)S(1)} %bitcast.32), kind=kOutput, calls=%fused_computation.4 | convolution fusion | flops 1619001344 | bytes 14954496 | tf_op jit(solution)/shard_map/pf,df->pd/dot_general | solution.py:126
  217.0 10.8 %all-to-all-start.1 = ((bf16[64,16,2048]{2,1,0:T(8,128)(2,1)}), bf16[64,16,2048]{2,1,0:T(8,128)(2,1)}, u32[]{:S(2)}, u32[]{:S(2)}) async-start(bf16[64,16,2048]{2,1,0:T(8,128)(2,1)} %bitcast.28), calls=%async_computation.2 | async-start | bytes 8388608 | tf_op jit(solution)/shard_map/all_to_all | solution.py:49
  227.8 3.9 %fusion.8 = f32[1,2048]{1,0:T(1,128)S(1)} fusion(f32[1024,1]{0,1:T(1,128)S(1)} %bitcast.33, bf16[1024,4096]{1,0:T(8,128)(2,1)} %all-gather.3.cloned.1.call-done), kind=kOutput, calls=%fused_computation.15 | convolution fusion | flops 25165824 | bytes 4206592 | tf_op jit(solution)/shard_map/dot_general | solution.py:122
  231.7 91.6 %all-to-all-done.1 = bf16[64,16,2048]{2,1,0:T(8,128)(2,1)} async-done(((bf16[64,16,2048]{2,1,0:T(8,128)(2,1)}), bf16[64,16,2048]{2,1,0:T(8,128)(2,1)}, u32[]{:S(2)}, u32[]{:S(2)}) %all-to-all-start.1) | async-done | bytes 4194336 | tf_op jit(solution)/shard_map/all_to_all | solution.py:49
  323.3 2.9 convert_reduce_fusion
  326.5 1.5 broadcast_in_dim.59
  328.0 5.9 %all-to-all-start.2 = ((f32[64,1,4097]{2,1,0:T(1,128)}), f32[64,1,4097]{2,1,0:T(1,128)S(1)}, u32[]{:S(2)}, u32[]{:S(2)}) async-start(f32[64,1,4097]{2,1,0:T(1,128)} %broadcast_in_dim.59), calls=%async_computation.3 | async-start | bytes 2162688 | tf_op jit(solution)/shard_map/all_to_all | solution.py:13
  334.0 2.1 convert_element_type.43
  336.1 13.2 %all_gather.19 = bf16[1024,384]{0,1:T(8,128)(2,1)} all-gather(bf16[256,384]{0,1:T(8,128)(2,1)} %get-tuple-element.9), channel_id=1, replica_groups=mesh['seq'=64,'tensor'=4] {'tensor'}, dimensions={0}, use_global_device_ids=true | all-gather | bytes 983040 | tf_op jit(solution)/shard_map/all_gather | solution.py:114
  349.3 10.4 %psum.7 = f32[16]{0:T(128)S(1)} all-reduce(f32[16]{0:T(128)S(1)} %get-tuple-element.8), channel_id=1, replica_groups=mesh['seq'=64,'tensor'=4] {'tensor'}, use_global_device_ids=true, to_apply=%region_6.8 | all-reduce | flops 16 | bytes 128 | tf_op jit(solution)/shard_map/psum | solution.py:131
  359.7 3.4 scatter_custom_fusion
  363.1 2.1 convert_element_type.51
  367.7 6.1 %multiply_convert_fusion.1 = bf16[2048,384]{1,0:T(8,128)(2,1)} fusion(bf16[1024,384]{0,1:T(8,128)(2,1)} %copy-done.3, bf16[1024,4096]{1,0:T(8,128)(2,1)} %all-gather.3.cloned.1.call-done, f32[]{:T(128)} %bitcast.11), kind=kOutput, calls=%fused_computation.11 | convolution fusion | flops 1612185600 | bytes 6554112 | tf_op jit(solution)/shard_map/pd,pf->df/dot_general | solution.py:120
  373.8 5.9 %multiply_convert_fusion.2 = bf16[2048,384]{1,0:T(8,128)(2,1)} fusion(bf16[1024,384]{0,1:T(8,128)(2,1)S(1)} %all_gather.16, bf16[1024,4096]{1,0:T(8,128)(2,1)} %all-gather.3.cloned.1.call-done, f32[]{:T(128)} %bitcast.11), kind=kOutput, calls=%fused_computation.12 | convolution fusion | flops 1612185600 | bytes 6554112 | tf_op jit(solution)/shard_map/pd,pf->df/dot_general | solution.py:119
  379.6 3.0 multiply_convert_fusion
  (46 shorter events, 6.9 us)
Async XLA Ops:
  7.2 104.6 %copy-start = (bf16[2048,384]{1,0:T(8,128)(2,1)S(1)}, bf16[2048,384]{1,0:T(8,128)(2,1)}, u32[]{:S(2)}) copy-start(bf16[2048,384]{1,0:T(8,128)(2,1)} %param.17) | copy-start | bytes 4718596
  11.8 9.2 %all-to-all-start = ((f32[4,1,16]{2,1,0:T(1,128)}), f32[4,1,16]{2,1,0:T(1,128)S(1)}, u32[]{:S(2)}, u32[]{:S(2)}) async-start(f32[4,1,16]{2,1,0:T(1,128)} %broadcast_in_dim.56), calls=%async_computation | async-start | bytes 4096 | tf_op jit(solution)/shard_map/all_to_all | solution.py:13
  17.3 89.9 %all-gather.3.cloned.1.call-start = ((), (), s32[]{:S(2)}) async-start(), calls=%async_computation.4 | async-start | bytes 8519680 | tf_op jit(solution)/shard_map/all_gather | solution.py:25
  22.5 146.8 %reduce-scatter.2.cloned.1.call-start = ((), (), s32[]{:S(2)}) async-start(), calls=%async_computation.5 | async-start | bytes 5939200 | tf_op jit(solution)/shard_map/reduce_scatter | solution.py:34
  107.1 5.1 %copy-start.1 = (bf16[1024,4096]{1,0:T(8,128)(2,1)S(1)}, bf16[1024,4096]{1,0:T(8,128)(2,1)}, u32[]{:S(2)}) copy-start(bf16[1024,4096]{1,0:T(8,128)(2,1)} %all-gather.3.cloned.1.call-done) | copy-start | bytes 25165828
  112.2 1.8 copy-start.7
  184.9 26.9 %copy-start.6 = (f32[2048]{0:T(1024)S(1)}, f32[2048]{0:T(1024)}, u32[]{:S(2)}) copy-start(f32[2048]{0:T(1024)} %param.16) | copy-start | bytes 24580
  184.9 26.9 %copy-start.8 = (bf16[2048,384]{1,0:T(8,128)(2,1)S(1)}, bf16[2048,384]{1,0:T(8,128)(2,1)}, u32[]{:S(2)}) copy-start(bf16[2048,384]{1,0:T(8,128)(2,1)} %param.18) | copy-start | bytes 4718596
  201.1 15.9 %copy-start.3 = (bf16[1024,384]{0,1:T(8,128)(2,1)}, bf16[1024,384]{0,1:T(8,128)(2,1)S(1)}, u32[]{:S(2)}) copy-start(bf16[1024,384]{0,1:T(8,128)(2,1)S(1)} %all_gather.17) | copy-start | bytes 2359300
  217.0 106.3 %all-to-all-start.1 = ((bf16[64,16,2048]{2,1,0:T(8,128)(2,1)}), bf16[64,16,2048]{2,1,0:T(8,128)(2,1)}, u32[]{:S(2)}, u32[]{:S(2)}) async-start(bf16[64,16,2048]{2,1,0:T(8,128)(2,1)} %bitcast.28), calls=%async_computation.2 | async-start | bytes 8388608 | tf_op jit(solution)/shard_map/all_to_all | solution.py:49
  227.8 98.4 %copy-start.5 = (f32[2048]{0:T(1024)S(1)}, f32[2048]{0:T(1024)}, u32[]{:S(2)}) copy-start(f32[2048]{0:T(1024)} %param.15) | copy-start | bytes 24580
  326.2 1.8 copy-start.2
  328.0 37.2 %all-to-all-start.2 = ((f32[64,1,4097]{2,1,0:T(1,128)}), f32[64,1,4097]{2,1,0:T(1,128)S(1)}, u32[]{:S(2)}, u32[]{:S(2)}) async-start(f32[64,1,4097]{2,1,0:T(1,128)} %broadcast_in_dim.59), calls=%async_computation.3 | async-start | bytes 2162688 | tf_op jit(solution)/shard_map/all_to_all | solution.py:13
  367.7 12.0 %slice-start = ((s8[8388608]{0:T(1024)(128)(4,1)}), s8[4194304]{0:T(1024)(128)(4,1)S(1)}, s32[]{:S(2)}) async-start(s8[8388608]{0:T(1024)(128)(4,1)} %bitcast.29), calls=%async_computation.6 | async-start | bytes 8388608
  373.7 5.9 %slice-start.1 = ((s8[8388608]{0:T(1024)(128)(4,1)}), s8[4194304]{0:T(1024)(128)(4,1)S(1)}, s32[]{:S(2)}) async-start(s8[8388608]{0:T(1024)(128)(4,1)} %bitcast.29), calls=%async_computation.7 | async-start | bytes 8388608
  373.8 5.9 %copy-start.4 = (bf16[1024,384]{0,1:T(8,128)(2,1)S(1)}, bf16[1024,384]{0,1:T(8,128)(2,1)}, u32[]{:S(2)}) copy-start(bf16[1024,384]{0,1:T(8,128)(2,1)} %all_gather.19) | copy-start | bytes 2359300
Sparse Core Ops, SparseCore 0:
  22.7 84.4 all-gather.2
  119.8 49.4 reduce-scatter.1
where the time goes:
time: 390 us; the launch traced here: 389 us
  waiting for transfers between devices  227 us (58%)
  blocking collectives  60.8 us (16%)
  matrix products  36 us (9%)
  starting transfers between devices  22.2 us (6%)
  other arithmetic  20.5 us (5%)
  between operations  15.6 us (4%)
  local copies, waits for them, and re-layouts  7.36 us (2%)
    all_to_all x1, waiting for transfers between devices, summed_on_arrival(): parts = lax.all_to_all(split_up(array, dim, count), axis, 0, 0, tiled=True)  91.6 us
    all_gather x1, waiting for transfers between devices, sent_together(): filled = lax.all_gather(both, axis, axis=dim, tiled=True)  83.8 us
    reduce_scatter x1, waiting for transfers between devices, in_one_piece(): filled = lax.psum_scatter(both, axis, scatter_dimension=dim, tiled=True)  49.6 us
    all_gather x1, blocking collectives, body(): lax.all_gather(d_up, 'tensor', axis=0, tiled=True)  13.8 us
    all_gather x1, blocking collectives, body(): lax.all_gather(weighted, 'tensor', axis=0, tiled=True)  13.2 us
    all_gather x1, blocking collectives, body(): lax.all_gather(d_gate, 'tensor', axis=0, tiled=True)  12.7 us
    all_to_all x2, starting transfers between devices, from_everyone(): lax.all_to_all(jnp.broadcast_to(array[None], (count, *array.shape)), axis...  11.4 us
    all_to_all x1, starting transfers between devices, summed_on_arrival(): parts = lax.all_to_all(split_up(array, dim, count), axis, 0, 0, tiled=True)  10.8 us
  transfers between devices with their start and end apart: 5, of which 4 were waited for; matrix products, arithmetic and copies ran while one was open for 4% of the time, Pallas kernels for 0%

commit v1 on v0

v1 whole, which is shorter than its diff:
```python
import functools

import jax
import jax.numpy as jnp
from jax import lax
from jax.experimental import pallas as pl
from jax.experimental.pallas import tpu as pltpu
from jax.sharding import PartitionSpec as P

MESH = pl.DeviceIdType.MESH
BF = jnp.bfloat16
F32 = jnp.float32
norm_eps = 1e-06
NC = 2
CAP = 16
AUX = 128
TOK = 128


def geometry(ny, nz, nx):
    s, t = lax.axis_index("seq"), lax.axis_index("tensor")
    c = lax.rem(s, NC)
    z = lax.rem(s // NC, nz)
    y = s // (NC * nz)
    way = 1 - 2 * c
    return y, z, c, t, way


def around(value, size):
    return lax.rem(value + 8 * size, size)


def step_of(k, way):
    far = (k + 1) // 2
    sign = (2 * lax.rem(k, 2) - 1) * way
    return sign, sign * far


def pair(value):
    high = value.astype(BF)
    return high, (value - high.astype(F32)).astype(BF)


def lanes(rows, columns):
    lane = lax.broadcasted_iota(jnp.int32, (rows, AUX), 1)
    total = jnp.zeros((rows, AUX), F32)
    for k, column in enumerate(columns):
        total = jnp.where(lane == k, jnp.broadcast_to(column, (rows, AUX)), total)
    return total


def dot(a, b, contract):
    return lax.dot_general(a, b, ((contract[0:1], contract[1:2]), ((), ())), preferred_element_type=F32)


def forward_kernel(
    sizes,
    tok, cnt, hid, gro, gain, rw, wg, wu, wd,
    N, U, G, scaled_o, inv_o,
    sq, sb, rb_a, rb_b, rb_s,
    sem_sq, sem_nz, sem_ny, sem_uz, sem_uy, sem_dn, sem_du,
    sem_a, sem_b, sem_s, sem_g1, sem_g2, sem_gs, sent,
):
    ny, nz, nx, width = sizes
    y, z, c, t, way = geometry(ny, nz, nx)
    wd_cols = hid.shape[1]
    ff = wg.shape[1]
    rows = NC * CAP

    def dev(yy, zz, cc, tt):
        return ((yy * nz + zz) * NC + cc, tt)

    def copy(src, dst, send, recv, to):
        return pltpu.make_async_remote_copy(
            src_ref=src, dst_ref=dst, send_sem=sent.at[send], recv_sem=recv, device_id=to, device_id_type=MESH
        )

    partner = dev(y, z, 1 - c, t)
    y_to = lambda d: dev(around(y + d, ny), z, c, t)
    z_to = lambda d: dev(y, around(z + d, nz), c, t)
    x_to = lambda d: dev(y, z, c, around(t + d, nx))

    barrier = pltpu.get_barrier_semaphore()
    for to in (y_to(1), y_to(-1), z_to(1), z_to(-1), partner, x_to(1), x_to(2), x_to(3)):
        pl.semaphore_signal(barrier, inc=1, device_id=to, device_id_type=MESH)

    hot = (tok[...] == lax.broadcasted_iota(jnp.int32, tok.shape, 1)).astype(F32).astype(BF)
    wide = dot(hot, hid[...], (1, 0))
    ups = dot(hot, gro[...], (1, 0))
    live = lax.broadcasted_iota(jnp.int32, (CAP, AUX), 0) < cnt[...]
    rounded = rw[...].astype(BF).astype(F32)
    s1 = jnp.sum(wide * wide, axis=1, keepdims=True)
    s2 = jnp.sum(wide * (gain[...] * rounded), axis=1, keepdims=True)
    sq[t] = lanes(CAP, (s1, s2))

    pl.semaphore_wait(barrier, 8)
    for d in (1, 2, 3):
        copy(sq.at[t], sq.at[t], 0, sem_sq.at[t], x_to(d)).start()
    U[z, y, c, :, 0:wd_cols] = jnp.where(live[:, 0:1], ups, 0.0).astype(BF)
    for d in (1, 2, 3):
        frm = around(t + d, nx)
        copy(sq.at[frm], sq.at[frm], 0, sem_sq.at[frm], x_to(1)).wait_recv()
    total = sq[0]
    for k in range(1, nx):
        total = total + sq[k]
    inverse = lax.rsqrt(total[:, 0:1] / width + norm_eps)
    scaled = wide * inverse
    N[z, y, c] = (scaled * gain[...]).astype(BF)
    scaled_o[...] = scaled
    inv_o[...] = jnp.broadcast_to(inverse, (CAP, AUX))
    high, low = pair(total[:, 1:2] * inverse)
    U[z, y, c, :, wd_cols:] = lanes(CAP, (high.astype(F32), low.astype(F32), cnt[:, 0:1].astype(F32))).astype(BF)

    def n_copy(zz, yy, send, recv, to):
        block = N.at[zz, yy, c]
        return copy(block, block, send, recv, to)

    def u_copy(zz, yy, send, recv, to):
        block = U.at[zz, yy, c]
        return copy(block, block, send, recv, to)

    def n_z_sends(yy):
        n_copy(z, yy, 2, sem_nz.at[1, yy], z_to(way)).start()
        if nz > 2:
            n_copy(z, yy, 2, sem_nz.at[2, yy], z_to(-way)).start()

    def u_y_sends(zz):
        u_copy(zz, y, 4, sem_uy.at[1, zz], y_to(way)).start()
        if ny > 2:
            u_copy(zz, y, 4, sem_uy.at[2, zz], y_to(-way)).start()

    n_copy(z, y, 1, sem_ny.at[1], y_to(way)).start()
    if ny > 2:
        n_copy(z, y, 1, sem_ny.at[2], y_to(-way)).start()
    u_copy(z, y, 3, sem_uz.at[1], z_to(way)).start()
    if nz > 2:
        u_copy(z, y, 3, sem_uz.at[2], z_to(-way)).start()
    n_z_sends(y)
    u_y_sends(z)

    for m in range(1, ny):
        sign, far = step_of(m, way)
        yy = around(y - far, ny)
        n_copy(z, yy, 1, sem_ny.at[m], y_to(sign)).wait_recv()
        if m + 2 < ny:
            n_copy(z, yy, 1, sem_ny.at[m + 2], y_to(sign)).start()
        n_z_sends(yy)
    copy(N.at[z, :, c], N.at[z, :, c], 5, sem_dn.at[z], partner).start()

    def chunk_z(k):
        return around(z - step_of(k, way)[1], nz)

    def u_y_arrival(k, m):
        zz = chunk_z(k)
        sign, far = step_of(m, way)
        yy = around(y - far, ny)
        u_copy(zz, yy, 4, sem_uy.at[m, zz], y_to(sign)).wait_recv()
        if m + 2 < ny:
            u_copy(zz, yy, 4, sem_uy.at[m + 2, zz], y_to(sign)).start()

    def x_block(i, d):
        return sb.at[i, around(t + d, nx)]

    def loop(k, carry):
        @pl.when((k >= 1) & (k < nz))
        def _():
            sign, far = step_of(k, way)
            zz = around(z - far, nz)
            to = z_to(sign)
            u_copy(zz, y, 3, sem_uz.at[k], to).wait_recv()

            @pl.when(k + 2 < nz)
            def _():
                u_copy(zz, y, 3, sem_uz.at[k + 2], to).start()

            u_y_sends(zz)
            for yy in range(ny):
                n_copy(zz, yy, 2, sem_nz.at[k, yy], to).wait_recv()

                @pl.when(k + 2 < nz)
                def _():
                    n_copy(zz, yy, 2, sem_nz.at[k + 2, yy], to).start()

            copy(N.at[zz, :, c], N.at[zz, :, c], 5, sem_dn.at[zz], partner).start()

        @pl.when((k >= 1) & (k - 1 < nz))
        def _():
            for m in range(1, min(ny, 3)):
                u_y_arrival(k - 1, m)

        @pl.when((k >= 2) & (k - 2 < nz))
        def _():
            for m in range(3, ny):
                u_y_arrival(k - 2, m)
            zz = chunk_z(k - 2)
            copy(U.at[zz, :, c], U.at[zz, :, c], 6, sem_du.at[zz], partner).start()

        @pl.when((k >= 4) & (k - 4 < nz))
        def _():
            i = k - 4
            block = x_block(i, way)
            copy(block, rb_a.at[i], 7, sem_a.at[i], x_to(way)).wait_recv()
            ref = sb.at[i, around(t + way, nx)]
            ref[...] = (ref[...].astype(F32) + rb_a[i].astype(F32)).astype(BF)
            copy(block, rb_b.at[i], 7, sem_b.at[i], x_to(way)).start()

        @pl.when((k >= 3) & (k - 3 < nz))
        def _():
            i = k - 3
            zz = chunk_z(i)
            other_n = N.at[zz, :, 1 - c]
            other_u = U.at[zz, :, 1 - c]
            copy(other_n, other_n, 5, sem_dn.at[zz], partner).wait_recv()
            copy(other_u, other_u, 6, sem_du.at[zz], partner).wait_recv()
            n = N[zz].reshape(ny * rows, wd_cols)
            u = U[zz, :, :, :, 0:wd_cols].reshape(ny * rows, wd_cols)
            for q, part in enumerate((dot(n, wg[...], (1, 0)), dot(n, wu[...], (1, 0)), dot(u, wd[...], (1, 1)))):
                sb[i, :, :, q * ff:(q + 1) * ff] = part.astype(BF).reshape(nx, rows, ff)
            copy(x_block(i, 2), rb_a.at[i], 7, sem_a.at[i], x_to(way)).start()
            copy(x_block(i, -way), rb_s.at[i], 7, sem_s.at[i], x_to(-way)).start()

        @pl.when((k >= 6) & (k - 6 < nz))
        def _():
            i = k - 6
            zz = chunk_z(i)
            block = G.at[zz, around(t - way, nx)]
            copy(block, block, 8, sem_g1.at[i], x_to(way)).wait_recv()
            copy(block, block, 8, sem_g2.at[i], x_to(way)).start()

        @pl.when((k >= 5) & (k - 5 < nz))
        def _():
            i = k - 5
            zz = chunk_z(i)
            block = x_block(i, 0)
            copy(block, rb_b.at[i], 7, sem_b.at[i], x_to(way)).wait_recv()
            copy(block, rb_s.at[i], 7, sem_s.at[i], x_to(-way)).wait_recv()
            full = sb[i, t].astype(F32) + rb_b[i].astype(F32) + rb_s[i].astype(F32)
            gate, upper, back = full[:, 0:ff], full[:, ff:2 * ff], full[:, 2 * ff:]
            aux = U[zz, t, :, :, wd_cols:].reshape(rows, AUX).astype(F32)
            logits = aux[:, 0:1] + aux[:, 1:2]
            sig = jax.nn.sigmoid(gate)
            act = gate * sig
            slope = sig * (1.0 + gate * (1.0 - sig))
            hidden = act * upper
            d_hidden = logits * back
            d_gate = (d_hidden * upper * slope).astype(BF)
            d_up = (d_hidden * act).astype(BF)
            router = jnp.sum(hidden * back, axis=1, keepdims=True)
            inner = jnp.sum(d_gate.astype(F32) * gate + d_up.astype(F32) * upper, axis=1, keepdims=True) + router * logits
            G[zz, t, :, 0:ff] = d_gate
            G[zz, t, :, ff:2 * ff] = d_up
            G[zz, t, :, 2 * ff:3 * ff] = (hidden * logits).astype(BF)
            rh, rl = pair(router)
            ih, il = pair(inner)
            G[zz, t, :, 3 * ff:] = lanes(rows, [v.astype(F32) for v in (rh, rl, ih, il)]).astype(BF)
            mine = G.at[zz, t]
            copy(mine, mine, 8, sem_g1.at[i], x_to(way)).start()
            copy(mine, mine, 8, sem_gs.at[i], x_to(-way)).start()

        @pl.when((k >= 7) & (k - 7 < nz))
        def _():
            i = k - 7
            zz = chunk_z(i)
            block = G.at[zz, around(t + way, nx)]
            copy(block, block, 8, sem_gs.at[i], x_to(way)).wait_recv()
            block = G.at[zz, around(t + 2, nx)]
            copy(block, block, 8, sem_g2.at[i], x_to(way)).wait_recv()

        return carry

    lax.fori_loop(0, nz + 7, loop, 0)

    def drain(ref, send):
        copy(ref, ref, send, sem_sq.at[0], partner).wait_send()

    drain(sq.at[0:3], 0)
    drain(N.at[0, 0:ny - 1, 0], 1)
    drain(N.at[0:nz - 1, :, 0], 2)
    drain(U.at[0:nz - 1, 0, 0], 3)
    drain(U.at[:, 0:ny - 1, 0], 4)
    drain(N.at[:, :, 0], 5)
    drain(U.at[:, :, 0], 6)
    drain(sb.at[:, 0:3], 7)
    drain(G.at[:, 0:3], 8)


def forward(sizes, tok, cnt, hid, gro, gain, rw, wg, wu, wd):
    ny, nz, nx, width = sizes
    cols, ff = wg.shape
    rows = NC * CAP
    vmem = pl.BlockSpec(memory_space=pltpu.VMEM)
    dma = pltpu.SemaphoreType.DMA
    return pl.pallas_call(
        functools.partial(forward_kernel, sizes),
        out_shape=(
            jax.ShapeDtypeStruct((nz, ny, NC, CAP, cols), BF),
            jax.ShapeDtypeStruct((nz, ny, NC, CAP, cols + AUX), BF),
            jax.ShapeDtypeStruct((nz, nx, rows, 3 * ff + AUX), BF),
            jax.ShapeDtypeStruct((CAP, cols), F32),
            jax.ShapeDtypeStruct((CAP, AUX), F32),
        ),
        in_specs=[vmem] * 9,
        out_specs=[vmem] * 5,
        scratch_shapes=[
            pltpu.VMEM((nx, CAP, AUX), F32),
            pltpu.VMEM((nz, nx, rows, 3 * ff), BF),
            pltpu.VMEM((nz, rows, 3 * ff), BF),
            pltpu.VMEM((nz, rows, 3 * ff), BF),
            pltpu.VMEM((nz, rows, 3 * ff), BF),
            dma((nx,)), dma((nz, ny)), dma((ny,)), dma((nz,)), dma((ny, nz)), dma((nz,)), dma((nz,)),
            dma((nz,)), dma((nz,)), dma((nz,)), dma((nz,)), dma((nz,)), dma((nz,)), dma((9,)),
        ],
        compiler_params=pltpu.CompilerParams(collective_id=0, has_side_effects=True, vmem_limit_bytes=64000000),
        name="forward",
    )(tok, cnt, hid, gro, gain, rw, wg, wu, wd)


def body(hidden_in, grad_out, slot_tokens, live_counts, norm_gain, router_weight, gate_weight, up_weight, down_weight, sizes):
    ny, nz, nx, width = sizes
    ff = gate_weight.shape[1]
    cols = hidden_in.shape[1]
    tok = jnp.broadcast_to(slot_tokens[:, None], (CAP, TOK))
    cnt = jnp.broadcast_to(live_counts[:, None], (CAP, AUX))
    N, U, G, scaled, inv = forward(
        sizes, tok, cnt, hidden_in, grad_out, norm_gain[None], router_weight[None], gate_weight, up_weight, down_weight
    )
    slots = nz * ny * NC * CAP
    n = N.reshape(slots, cols)
    u = U[..., :cols].reshape(slots, cols)
    aux = G[..., 3 * ff:].astype(F32)
    g = G.reshape(slots, -1)
    d_gate, d_up, weighted = g[:, :ff], g[:, ff:2 * ff], g[:, 2 * ff:3 * ff]
    rg = (aux[..., 0] + aux[..., 1]).reshape(slots)
    count_scale = lax.rsqrt(jnp.sum(U[:, :, :, 0, cols + 2].astype(F32)))
    grad_gate = jnp.einsum("pd,pf->df", n, d_gate, preferred_element_type=F32)
    grad_up = jnp.einsum("pd,pf->df", n, d_up, preferred_element_type=F32)
    grad_down = jnp.einsum("pf,pd->fd", weighted, u, preferred_element_type=F32)
    router_part = jnp.dot(rg, n.astype(F32), precision=lax.Precision.HIGHEST)
    total = jnp.einsum("pf,df->pd", d_gate, gate_weight, preferred_element_type=F32)
    total = total + jnp.einsum("pf,df->pd", d_up, up_weight, preferred_element_type=F32)
    total = (total + rg[:, None] * router_weight).astype(BF)
    parts = jnp.moveaxis(total.reshape(nz, ny, NC, CAP, cols), 0, 1).reshape(-1, CAP, cols)
    d_normed = lax.all_to_all(parts, "seq", 0, 0, tiled=True).astype(F32).sum(axis=0)
    d_scaled = d_normed * norm_gain
    inner = lax.psum(jnp.sum(d_scaled * scaled, axis=1), "tensor") / width
    live = lax.iota(jnp.int32, CAP) < live_counts[0]
    d_picked = inv[:, 0:1] * (d_scaled - scaled * inner[:, None])
    d_picked = jnp.where(live[:, None], d_picked, 0.0)
    sums = lax.psum(jnp.concatenate([jnp.sum(d_normed * scaled, axis=0), router_part]), "seq")
    grad_in = grad_out.astype(F32).at[slot_tokens].add(d_picked).astype(BF)
    return (
        grad_in,
        (count_scale * grad_gate).astype(BF),
        (count_scale * grad_up).astype(BF),
        (count_scale * grad_down).astype(BF),
        count_scale * sums[:cols],
        count_scale * sums[cols:],
    )


def solution(mesh):
    nx = mesh.shape["tensor"]
    ny = nx
    nz = mesh.shape["seq"] // (ny * NC)
    weights = (P("tensor", "seq"), P("tensor", "seq"), P("seq", "tensor"))
    in_specs = (P("seq", "tensor"), P("seq", "tensor"), P("seq"), P("seq"), P("tensor"), P("tensor")) + weights
    out_specs = (P("seq", "tensor"),) + weights + (P("tensor"), P("tensor"))

    def whole(hidden_in, *rest):
        sizes = (ny, nz, nx, hidden_in.shape[1] * nx)
        return body(hidden_in, *rest, sizes)

    return jax.shard_map(whole, mesh=mesh, in_specs=in_specs, out_specs=out_specs, check_vma=False)
```

time: 390 us -> 473 us (1.21)
  blocking collectives: 60.8 us -> 255 us
  waiting for transfers between devices: 227 us -> 72.4 us
  Pallas kernels: 0 us -> 94 us
  starting transfers between devices: 22.2 us -> 8.33 us
  between operations: 15.6 us -> 2.12 us
  matrix products: 36 us -> 22.8 us
  other arithmetic: 20.5 us -> 8.92 us
    psum x1 -> x2, blocking collectives: 10.4 us -> 255 us  [the longest x1 246 us: body(): lax.psum(jnp.concatenate([jnp.sum(d_normed * scaled, axis=0), router_part...]
    pallas_call x0 -> x1, Pallas kernels: none -> 94 us  [forward(): pl.pallas_call(functools.partial(forward_kernel, sizes), out_shape=(jax.S...]
    all_gather x1 -> x0, waiting for transfers between devices: 83.8 us -> none  [sent_together(): filled = lax.all_gather(both, axis, axis=dim, tiled=True)]
    all_gather x4 -> x0, blocking collectives: 50.3 us -> none  [the longest x1 13.8 us: body(): lax.all_gather(d_up, 'tensor', axis=0, tiled=True)]
    reduce_scatter x1 -> x0, waiting for transfers between devices: 49.6 us -> none  [in_one_piece(): filled = lax.psum_scatter(both, axis, scatter_dimension=dim, tiled=True)]
    all_to_all x3 -> x1, waiting for transfers between devices: 93.5 us -> 72.4 us  [body(): lax.all_to_all(parts, 'seq', 0, 0, tiled=True).astype(F32).sum(axis=0)]
    all_to_all x3 -> x1, starting transfers between devices: 22.1 us -> 8.33 us  [body(): lax.all_to_all(parts, 'seq', 0, 0, tiled=True).astype(F32).sum(axis=0)]
    dot_general x10 -> x6, matrix products: 36 us -> 22.8 us  [the longest x1 4.29 us: body(): grad_down = jnp.einsum('pf,pd->fd', weighted, u, preferred_element_type=F32)]
  transfers between devices with their start and end apart: 5 -> 1, of which waited for: 4 -> 1; matrix products, arithmetic and copies ran while one was open for 4% -> 5% of each run, Pallas kernels for 0% -> 0%
where the time goes in v1:
time: 473 us
  blocking collectives  255 us (54%)
  Pallas kernels  94 us (20%)
  waiting for transfers between devices  72.4 us (15%)
  matrix products  22.8 us (5%)
  local copies, waits for them, and re-layouts  9.23 us (2%)
  other arithmetic  8.92 us (2%)
  starting transfers between devices  8.33 us (2%)
    psum x1, blocking collectives, body(): lax.psum(jnp.concatenate([jnp.sum(d_normed * scaled, axis=0), router_part...  246 us
    pallas_call x1, Pallas kernels, forward(): pl.pallas_call(functools.partial(forward_kernel, sizes), out_shape=(jax.S...  94 us
    all_to_all x1, waiting for transfers between devices, body(): lax.all_to_all(parts, 'seq', 0, 0, tiled=True).astype(F32).sum(axis=0)  72.4 us
  transfers between devices with their start and end apart: 1, of which 1 were waited for; matrix products, arithmetic and copies ran while one was open for 5% of the time, Pallas kernels for 0%

profile of v1, /device:TPU:2, one launch (start us, length us, event | category | flops | bytes accessed | tf_op | source)
XLA Modules:
  0.0 472.9 jit_solution(13141164297318111690)
XLA Ops:
  1.3 1.3 broadcast_in_dim.39.tok
  2.6 0.6 broadcast_in_dim.40.cnt
  3.2 94.0 %forward.1 = (bf16[8,4,2,16,2048]{4,3,2,1,0:T(8,128)(2,1)}, bf16[8,4,2,16,2176]{4,3,2,1,0:T(8,128)(2,1)}, bf16[8,4,32,1280]{3,2,1,0:T(8,128)(2,1)}, f32[16,2048]{1,0:T(8,128)}, f32[16,128]{1,0:T(8,128)}) custom-call(s32[16,128]{1,0:T(8,128)} %broadcast_in_dim.39.tok, s32[16,128]{1,0:T(8,128)} %broadcast_in_dim.40.cnt, bf16[128,2048]{1,0:T(8,128)(2,1)} %hid.1, ...), custom_call_target="tpu_custom_call" | custom-call | tf_op jit(solution)/shard_map/forward/pallas_call | solution.py:293
  97.2 1.0 slice_convert_fusion
  98.3 0.4 fusion.6
  98.7 0.1 add.30
  98.8 0.0 copy-done
  98.8 3.6 fusion.4
  102.4 0.0 copy-done.4
  102.4 3.6 add_convert_fusion
  106.0 2.2 copy.15
  108.3 8.3 %all-to-all-start = ((bf16[64,16,2048]{2,1,0:T(8,128)(2,1)}), bf16[64,16,2048]{2,1,0:T(8,128)(2,1)}, u32[]{:S(2)}, u32[]{:S(2)}) async-start(bf16[64,16,2048]{2,1,0:T(8,128)(2,1)} %bitcast.20), calls=%async_computation | async-start | bytes 8388608 | tf_op jit(solution)/shard_map/all_to_all | solution.py:343
  116.6 0.1 convert_element_type.29
  116.7 0.1 reshape.65
  116.8 4.8 %slice.41 = bf16[8,4,2,16,2048]{4,3,2,1,0:T(8,128)(2,1)} slice(bf16[8,4,2,16,2176]{4,3,2,1,0:T(8,128)(2,1)} %get-tuple-element.14), slice={[0:8], [0:4], [0:2], [0:16], [0:2048]} | slice | bytes 8388608 | tf_op jit(solution)/shard_map/slice | solution.py:329
  121.6 1.6 convert_reduce_fusion.1
  124.0 0.1 slice_reduce_fusion
  124.1 0.0 copy-done.10
  124.1 4.1 fusion.18
  128.2 0.0 copy-start.5
  128.2 4.3 multiply_convert_fusion
  132.5 0.0 copy-done.1
  132.5 3.6 multiply_convert_fusion.1
  136.0 3.6 multiply_convert_fusion.2
  139.6 72.4 %all-to-all-done = bf16[64,16,2048]{2,1,0:T(8,128)(2,1)} async-done(((bf16[64,16,2048]{2,1,0:T(8,128)(2,1)}), bf16[64,16,2048]{2,1,0:T(8,128)(2,1)}, u32[]{:S(2)}, u32[]{:S(2)}) %all-to-all-start) | async-done | bytes 4194336 | tf_op jit(solution)/shard_map/all_to_all | solution.py:343
  212.0 2.9 convert_reduce_fusion
  214.9 0.2 multiply_reduce_fusion
  215.1 246.4 %psum.15 = f32[4096]{0:T(1024)S(1)} all-reduce(f32[4096]{0:T(1024)S(1)} %pad_maximum_fusion), channel_id=1, replica_groups=mesh['seq'=64,'tensor'=4] {'seq'}, use_global_device_ids=true, to_apply=%region_6.7 | all-reduce | flops 4096 | bytes 32768 | tf_op jit(solution)/shard_map/psum | solution.py:349
  461.4 0.6 slice_multiply_fusion
  462.0 8.7 %psum.14 = f32[16]{0:T(128)S(1)} all-reduce(f32[16]{0:T(128)S(1)} %get-tuple-element.17), channel_id=1, replica_groups=mesh['seq'=64,'tensor'=4] {'tensor'}, use_global_device_ids=true, to_apply=%region_2.0 | all-reduce | flops 16 | bytes 128 | tf_op jit(solution)/shard_map/psum | solution.py:345
  470.8 1.3 scatter_custom_fusion
  472.0 0.9 convert_element_type.33
  (21 shorter events, 0.0 us)
Async XLA Ops:
  3.2 95.5 %copy-start = (bf16[2048,384]{1,0:T(8,128)(2,1)S(1)}, bf16[2048,384]{1,0:T(8,128)(2,1)}, u32[]{:S(2)}) copy-start(bf16[2048,384]{1,0:T(8,128)(2,1)} %wg.1) | copy-start | bytes 4718596
  98.8 3.6 copy-start.4
  98.8 3.7 copy-start.8
  108.3 8.3 %copy-start.3 = (bf16[128,2048]{1,0:T(8,128)(2,1)S(1)}, bf16[128,2048]{1,0:T(8,128)(2,1)}, u32[]{:S(2)}) copy-start(bf16[128,2048]{1,0:T(8,128)(2,1)} %gro.1) | copy-start | bytes 1572868
  108.3 103.7 %all-to-all-start = ((bf16[64,16,2048]{2,1,0:T(8,128)(2,1)}), bf16[64,16,2048]{2,1,0:T(8,128)(2,1)}, u32[]{:S(2)}, u32[]{:S(2)}) async-start(bf16[64,16,2048]{2,1,0:T(8,128)(2,1)} %bitcast.20), calls=%async_computation | async-start | bytes 8388608 | tf_op jit(solution)/shard_map/all_to_all | solution.py:343
  116.8 7.1 %copy-start.9 = (f32[16,128]{1,0:T(8,128)S(1)}, f32[16,128]{1,0:T(8,128)}, u32[]{:S(2)}) copy-start(f32[16,128]{1,0:T(8,128)} %get-tuple-element.11) | copy-start | bytes 24580
  116.8 7.2 %copy-start.10 = (s32[16]{0:T(128)S(1)}, s32[16]{0:T(128)}, u32[]{:S(2)}) copy-start(s32[16]{0:T(128)} %param.11) | copy-start | bytes 196
  123.9 4.2 copy-start.2
  128.2 4.3 copy-start.1
  128.2 4.3 copy-start.5
  139.6 75.2 %copy-start.6 = (f32[16,2048]{1,0:T(8,128)S(1)}, f32[16,2048]{1,0:T(8,128)}, u32[]{:S(2)}) copy-start(f32[16,2048]{1,0:T(8,128)} %get-tuple-element.13) | copy-start | bytes 393220
  139.6 75.3 %copy-start.7 = (f32[2048]{0:T(1024)S(1)}, f32[2048]{0:T(1024)}, u32[]{:S(2)}) copy-start(f32[2048]{0:T(1024)} %param.13) | copy-start | bytes 24580

commit v2 on v1

--- a/solution.py
+++ b/solution.py
@@ -15,6 +15,7 @@
 CAP = 16
 AUX = 128
 TOK = 128
+TILE = 256
 
 
 def geometry(ny, nz, nx):
@@ -53,13 +54,16 @@
     return lax.dot_general(a, b, ((contract[0:1], contract[1:2]), ((), ())), preferred_element_type=F32)
 
 
-def forward_kernel(
+def kernel(
     sizes,
-    tok, cnt, hid, gro, gain, rw, wg, wu, wd,
+    tok, tok_row, cnt, hid, gro, gain, rw, wg, wu, wd,
+    grad_in, grad_gate, grad_up, grad_down, grad_gain, grad_router,
     N, U, G, scaled_o, inv_o,
     sq, sb, rb_a, rb_b, rb_s,
+    t_a, t_b, acc_a, acc_b, a1l, a1s, a2l, a2s, b1l, b1s, b2l, b2s, v_acc, v_own, v_core, v_y, v_z,
     sem_sq, sem_nz, sem_ny, sem_uz, sem_uy, sem_dn, sem_du,
-    sem_a, sem_b, sem_s, sem_g1, sem_g2, sem_gs, sent,
+    sem_a, sem_b, sem_s, sem_g1, sem_g2, sem_gs,
+    sem_ta, sem_tb, sem_a1, sem_a2, sem_b1, sem_b2, sem_v, sem_vy, sem_vz, sent,
 ):
     ny, nz, nx, width = sizes
     y, z, c, t, way = geometry(ny, nz, nx)
@@ -81,7 +85,8 @@
     x_to = lambda d: dev(y, z, c, around(t + d, nx))
 
     barrier = pltpu.get_barrier_semaphore()
-    for to in (y_to(1), y_to(-1), z_to(1), z_to(-1), partner, x_to(1), x_to(2), x_to(3)):
+    peers = [y_to(d) for d in range(1, ny)] + [z_to(d) for d in range(1, nz)] + [x_to(d) for d in range(1, nx)] + [partner]
+    for to in peers:
         pl.semaphore_signal(barrier, inc=1, device_id=to, device_id_type=MESH)
 
     hot = (tok[...] == lax.broadcasted_iota(jnp.int32, tok.shape, 1)).astype(F32).astype(BF)
@@ -93,7 +98,7 @@
     s2 = jnp.sum(wide * (gain[...] * rounded), axis=1, keepdims=True)
     sq[t] = lanes(CAP, (s1, s2))
 
-    pl.semaphore_wait(barrier, 8)
+    pl.semaphore_wait(barrier, len(peers))
     for d in (1, 2, 3):
         copy(sq.at[t], sq.at[t], 0, sem_sq.at[t], x_to(d)).start()
     U[z, y, c, :, 0:wd_cols] = jnp.where(live[:, 0:1], ups, 0.0).astype(BF)
@@ -270,6 +275,157 @@
 
     lax.fori_loop(0, nz + 7, loop, 0)
 
+    half = wd_cols // 2
+
+    v_acc[...] = jnp.zeros_like(v_acc)
+
+    def partial(i, carry):
+        zz = around(z + nz // 2 + i, nz)
+        g = G[zz].reshape(ny * rows, 3 * ff + AUX)
+        out = dot(g[:, 0:ff], wg[...], (1, 1)) + dot(g[:, ff:2 * ff], wu[...], (1, 1))
+        n = N[zz].reshape(ny * rows, wd_cols).astype(F32)
+        aux = g[:, 3 * ff:].astype(F32)
+        router = aux[:, 0:1] + aux[:, 1:2]
+        v_acc[0] += jnp.sum((out * n).reshape(-1, 8, wd_cols), axis=0)
+        v_acc[1] += jnp.sum((n * router).reshape(-1, 8, wd_cols), axis=0)
+        out = out.astype(BF)
+        t_a[:, zz, :, :, 0:half] = out[:, 0:half].reshape(ny, NC, CAP, half)
+        t_a[:, zz, :, :, half:] = g[:, 3 * ff:].reshape(ny, NC, CAP, AUX)
+        t_b[zz] = out[:, half:].reshape(ny, NC, CAP, half)
+        copy(t_a.at[:, zz, 1 - c], acc_a.at[:, zz], 9, sem_ta.at[zz], partner).start()
+        copy(t_b.at[zz, :, 1 - c], acc_b.at[zz], 10, sem_tb.at[zz], partner).start()
+        return carry
+
+    lax.fori_loop(0, nz, partial, 0)
+
+    v_own[...] = jnp.sum(v_acc[...], axis=1)
+    v_own_copy = copy(v_own, v_core, 15, sem_v.at[0], partner)
+    v_own_copy.start()
+
+    def combine(i, carry):
+        zz = around(z + nz // 2 + i, nz)
+        copy(t_a.at[:, zz, 1 - c], acc_a.at[:, zz], 9, sem_ta.at[zz], partner).wait_recv()
+        copy(t_b.at[zz, :, 1 - c], acc_b.at[zz], 10, sem_tb.at[zz], partner).wait_recv()
+        acc_a[:, zz] = (acc_a[:, zz].astype(F32) + t_a[:, zz, c].astype(F32)).astype(BF)
+        acc_b[zz] = (acc_b[zz].astype(F32) + t_b[zz, :, c].astype(F32)).astype(BF)
+        return carry
+
+    lax.fori_loop(0, nz, combine, 0)
+
+    def ring(n, at, get, left, right, sems, send, to):
+        top = n // 2
+
+        def add(ref, other):
+            ref[...] = (ref[...].astype(F32) + other[...].astype(F32)).astype(BF)
+
+        def start():
+            copy(get(around(at + top * way, n)), left.at[top - 1], send, sems.at[0, top - 1], to(way)).start()
+            if top > 1:
+                copy(get(around(at - (top - 1) * way, n)), right.at[top - 2], send, sems.at[1, top - 2], to(-way)).start()
+
+        def step(r):
+            ref = get(around(at + r * way, n))
+            copy(ref, left.at[r], send, sems.at[0, r], to(way)).wait_recv()
+            add(ref, left.at[r])
+            if r > 0:
+                copy(ref, left.at[r - 1], send, sems.at[0, r - 1], to(way)).start()
+                q = r - 1
+                ref = get(around(at - q * way, n))
+                copy(ref, right.at[q], send, sems.at[1, q], to(-way)).wait_recv()
+                add(ref, right.at[q])
+                if q > 0:
+                    copy(ref, right.at[q - 1], send, sems.at[1, q - 1], to(-way)).start()
+
+        return start, [functools.partial(step, r) for r in range(top - 1, -1, -1)]
+
+    a1_start, a1 = ring(ny, y, lambda p: acc_a.at[p], a1l, a1s, sem_a1, 11, y_to)
+    a2_start, a2 = ring(nz, z, lambda p: acc_a.at[y, p], a2l, a2s, sem_a2, 12, z_to)
+    b1_start, b1 = ring(nz, z, lambda p: acc_b.at[p], b1l, b1s, sem_b1, 13, z_to)
+    b2_start, b2 = ring(ny, y, lambda p: acc_b.at[z, p], b2l, b2s, sem_b2, 14, y_to)
+
+    def then(first, second):
+        def both():
+            first()
+            second()
+
+        return both
+
+    a_steps = a1[:-1] + [then(a1[-1], a2_start)] + a2
+    b_steps = b1[:-1] + [then(b1[-1], b2_start)] + b2
+
+    def v_copy(ref, sem, send, to):
+        return copy(ref, ref, send, sem, to)
+
+    def v_first():
+        v_own_copy.wait_recv()
+        v_y[y] = v_own[...] + v_core[...]
+        for d in range(1, ny):
+            v_copy(v_y.at[y], sem_vy.at[y], 16, y_to(d)).start()
+
+    def v_second():
+        for d in range(1, ny):
+            frm = around(y + d, ny)
+            v_copy(v_y.at[frm], sem_vy.at[frm], 16, y_to(d)).wait_recv()
+        total = v_y[0]
+        for k in range(1, ny):
+            total = total + v_y[k]
+        v_z[z] = total
+        for d in range(1, nz):
+            v_copy(v_z.at[z], sem_vz.at[z], 17, z_to(d)).start()
+
+    a1_start()
+    b1_start()
+    counts = U[:, :, :, :, wd_cols:].reshape(-1, AUX).astype(F32)
+    count_scale = lax.rsqrt(jnp.sum(counts, axis=0, keepdims=True)[:, 2:3] / CAP)
+
+    tiles = wd_cols // TILE
+    schedule = {}
+    for k, pick in enumerate(zip(a_steps, b_steps)):
+        schedule[k] = list(pick)
+    schedule[0].insert(0, v_first)
+    schedule[1].insert(0, v_second)
+    lag = max(tiles - len(schedule), 0)
+
+    def tile(i, carry):
+        columns = pl.ds(pl.multiple_of(i * TILE, TILE), TILE)
+        slots = ny * nz * rows
+        n = N[:, :, :, :, columns].reshape(slots, TILE)
+        u = U[:, :, :, :, columns].reshape(slots, TILE)
+        g = G[:, :, :, 0:3 * ff].reshape(slots, 3 * ff)
+        both = (dot(n, g[:, 0:2 * ff], (0, 0)) * count_scale).astype(BF)
+        grad_gate[columns] = both[:, 0:ff]
+        grad_up[columns] = both[:, ff:]
+        grad_down[:, columns] = (dot(g[:, 2 * ff:], u, (0, 0)) * count_scale).astype(BF)
+        for k, picks in schedule.items():
+            @pl.when(i == k + lag)
+            def _():
+                for pick in picks:
+                    pick()
+        return carry
+
+    lax.fori_loop(0, max(tiles, len(schedule)), tile, 0)
+
+    for d in range(1, nz):
+        frm = around(z + d, nz)
+        v_copy(v_z.at[frm], sem_vz.at[frm], 17, z_to(d)).wait_recv()
+    sums = v_z[0]
+    for k in range(1, nz):
+        sums = sums + v_z[k]
+    gain_sum, router_sum = sums[0:1], sums[1:2]
+    grad_router[...] = count_scale * router_sum
+    grad_gain[...] = count_scale * ((gain_sum + rw[...] * router_sum) / gain[...])
+
+    mine = acc_a[y, z].astype(F32)
+    router = mine[:, half:half + 1] + mine[:, half + 1:half + 2]
+    inner = (mine[:, half + 2:half + 3] + mine[:, half + 3:half + 4]) / width
+    d_normed = jnp.concatenate([mine[:, 0:half], acc_b[z, y].astype(F32)], axis=1) + router * rw[...]
+    live = lax.broadcasted_iota(jnp.int32, (CAP, AUX), 0) < cnt[...]
+    d_picked = inv_o[:, 0:1] * (d_normed * gain[...] - scaled_o[...] * inner)
+    d_picked = jnp.where(live[:, 0:1], d_picked, 0.0)
+    spread = (lax.broadcasted_iota(jnp.int32, (TOK, CAP), 0) == tok_row[...]).astype(F32).astype(BF)
+    high, low = pair(d_picked)
+    grad_in[...] = (gro[...].astype(F32) + dot(spread, high, (1, 0)) + dot(spread, low, (1, 0))).astype(BF)
+
     def drain(ref, send):
         copy(ref, ref, send, sem_sq.at[0], partner).wait_send()
 
@@ -282,80 +438,84 @@
     drain(U.at[:, :, 0], 6)
     drain(sb.at[:, 0:3], 7)
     drain(G.at[:, 0:3], 8)
-
-
-def forward(sizes, tok, cnt, hid, gro, gain, rw, wg, wu, wd):
+    drain(acc_a, 9)
+    drain(acc_b, 10)
+    drain(acc_a.at[0:ny - 1], 11)
+    drain(acc_a.at[0, 0:nz - 1], 12)
+    drain(acc_b.at[0:nz - 1], 13)
+    drain(acc_b.at[0, 0:ny - 1], 14)
+    drain(v_own, 15)
+    drain(v_y.at[0:ny - 1], 16)
+    drain(v_z.at[0:nz - 1], 17)
+
+
+def body(hidden_in, grad_out, slot_tokens, live_counts, norm_gain, router_weight, gate_weight, up_weight, down_weight, sizes):
     ny, nz, nx, width = sizes
-    cols, ff = wg.shape
+    cols, ff = gate_weight.shape
     rows = NC * CAP
+    half = cols // 2
     vmem = pl.BlockSpec(memory_space=pltpu.VMEM)
     dma = pltpu.SemaphoreType.DMA
-    return pl.pallas_call(
-        functools.partial(forward_kernel, sizes),
+    scratch = pltpu.VMEM
+
+    def slots(n):
+        return n // 2, max(n // 2 - 1, 1)
+
+    yl, ys = slots(ny)
+    zl, zs = slots(nz)
+    a, b = half + AUX, half
+    tok = jnp.broadcast_to(slot_tokens[:, None], (CAP, TOK))
+    tok_row = jnp.broadcast_to(slot_tokens[None], (TOK, CAP))
+    cnt = jnp.broadcast_to(live_counts[:, None], (CAP, AUX))
+    grad_in, grad_gate, grad_up, grad_down, grad_gain, grad_router = pl.pallas_call(
+        functools.partial(kernel, sizes),
         out_shape=(
-            jax.ShapeDtypeStruct((nz, ny, NC, CAP, cols), BF),
-            jax.ShapeDtypeStruct((nz, ny, NC, CAP, cols + AUX), BF),
-            jax.ShapeDtypeStruct((nz, nx, rows, 3 * ff + AUX), BF),
-            jax.ShapeDtypeStruct((CAP, cols), F32),
-            jax.ShapeDtypeStruct((CAP, AUX), F32),
+            jax.ShapeDtypeStruct(grad_out.shape, BF),
+            jax.ShapeDtypeStruct((cols, ff), BF),
+            jax.ShapeDtypeStruct((cols, ff), BF),
+            jax.ShapeDtypeStruct((ff, cols), BF),
+            jax.ShapeDtypeStruct((1, cols), F32),
+            jax.ShapeDtypeStruct((1, cols), F32),
         ),
-        in_specs=[vmem] * 9,
-        out_specs=[vmem] * 5,
+        in_specs=[vmem] * 10,
+        out_specs=[vmem] * 6,
         scratch_shapes=[
-            pltpu.VMEM((nx, CAP, AUX), F32),
-            pltpu.VMEM((nz, nx, rows, 3 * ff), BF),
-            pltpu.VMEM((nz, rows, 3 * ff), BF),
-            pltpu.VMEM((nz, rows, 3 * ff), BF),
-            pltpu.VMEM((nz, rows, 3 * ff), BF),
+            scratch((nz, ny, NC, CAP, cols), BF),
+            scratch((nz, ny, NC, CAP, cols + AUX), BF),
+            scratch((nz, nx, rows, 3 * ff + AUX), BF),
+            scratch((CAP, cols), F32),
+            scratch((CAP, AUX), F32),
+            scratch((nx, CAP, AUX), F32),
+            scratch((nz, nx, rows, 3 * ff), BF),
+            scratch((nz, rows, 3 * ff), BF),
+            scratch((nz, rows, 3 * ff), BF),
+            scratch((nz, rows, 3 * ff), BF),
+            scratch((ny, nz, NC, CAP, a), BF),
+            scratch((nz, ny, NC, CAP, b), BF),
+            scratch((ny, nz, CAP, a), BF),
+            scratch((nz, ny, CAP, b), BF),
+            scratch((yl, nz, CAP, a), BF),
+            scratch((ys, nz, CAP, a), BF),
+            scratch((zl, CAP, a), BF),
+            scratch((zs, CAP, a), BF),
+            scratch((zl, ny, CAP, b), BF),
+            scratch((zs, ny, CAP, b), BF),
+            scratch((yl, CAP, b), BF),
+            scratch((ys, CAP, b), BF),
+            scratch((2, 8, cols), F32),
+            scratch((2, cols), F32),
+            scratch((2, cols), F32),
+            scratch((ny, 2, cols), F32),
+            scratch((nz, 2, cols), F32),
             dma((nx,)), dma((nz, ny)), dma((ny,)), dma((nz,)), dma((ny, nz)), dma((nz,)), dma((nz,)),
-            dma((nz,)), dma((nz,)), dma((nz,)), dma((nz,)), dma((nz,)), dma((nz,)), dma((9,)),
+            dma((nz,)), dma((nz,)), dma((nz,)), dma((nz,)), dma((nz,)), dma((nz,)),
+            dma((nz,)), dma((nz,)), dma((2, yl)), dma((2, zl)), dma((2, zl)), dma((2, yl)), dma((1,)), dma((ny,)), dma((nz,)),
+            dma((18,)),
         ],
-        compiler_params=pltpu.CompilerParams(collective_id=0, has_side_effects=True, vmem_limit_bytes=64000000),
-        name="forward",
-    )(tok, cnt, hid, gro, gain, rw, wg, wu, wd)
-
-
-def body(hidden_in, grad_out, slot_tokens, live_counts, norm_gain, router_weight, gate_weight, up_weight, down_weight, sizes):
-    ny, nz, nx, width = sizes
-    ff = gate_weight.shape[1]
-    cols = hidden_in.shape[1]
-    tok = jnp.broadcast_to(slot_tokens[:, None], (CAP, TOK))
-    cnt = jnp.broadcast_to(live_counts[:, None], (CAP, AUX))
-    N, U, G, scaled, inv = forward(
-        sizes, tok, cnt, hidden_in, grad_out, norm_gain[None], router_weight[None], gate_weight, up_weight, down_weight
-    )
-    slots = nz * ny * NC * CAP
-    n = N.reshape(slots, cols)
-    u = U[..., :cols].reshape(slots, cols)
-    aux = G[..., 3 * ff:].astype(F32)
-    g = G.reshape(slots, -1)
-    d_gate, d_up, weighted = g[:, :ff], g[:, ff:2 * ff], g[:, 2 * ff:3 * ff]
-    rg = (aux[..., 0] + aux[..., 1]).reshape(slots)
-    count_scale = lax.rsqrt(jnp.sum(U[:, :, :, 0, cols + 2].astype(F32)))
-    grad_gate = jnp.einsum("pd,pf->df", n, d_gate, preferred_element_type=F32)
-    grad_up = jnp.einsum("pd,pf->df", n, d_up, preferred_element_type=F32)
-    grad_down = jnp.einsum("pf,pd->fd", weighted, u, preferred_element_type=F32)
-    router_part = jnp.dot(rg, n.astype(F32), precision=lax.Precision.HIGHEST)
-    total = jnp.einsum("pf,df->pd", d_gate, gate_weight, preferred_element_type=F32)
-    total = total + jnp.einsum("pf,df->pd", d_up, up_weight, preferred_element_type=F32)
-    total = (total + rg[:, None] * router_weight).astype(BF)
-    parts = jnp.moveaxis(total.reshape(nz, ny, NC, CAP, cols), 0, 1).reshape(-1, CAP, cols)
-    d_normed = lax.all_to_all(parts, "seq", 0, 0, tiled=True).astype(F32).sum(axis=0)
-    d_scaled = d_normed * norm_gain
-    inner = lax.psum(jnp.sum(d_scaled * scaled, axis=1), "tensor") / width
-    live = lax.iota(jnp.int32, CAP) < live_counts[0]
-    d_picked = inv[:, 0:1] * (d_scaled - scaled * inner[:, None])
-    d_picked = jnp.where(live[:, None], d_picked, 0.0)
-    sums = lax.psum(jnp.concatenate([jnp.sum(d_normed * scaled, axis=0), router_part]), "seq")
-    grad_in = grad_out.astype(F32).at[slot_tokens].add(d_picked).astype(BF)
-    return (
-        grad_in,
-        (count_scale * grad_gate).astype(BF),
-        (count_scale * grad_up).astype(BF),
-        (count_scale * grad_down).astype(BF),
-        count_scale * sums[:cols],
-        count_scale * sums[cols:],
-    )
+        compiler_params=pltpu.CompilerParams(collective_id=0, has_side_effects=True, vmem_limit_bytes=67000000),
+        name="block",
+    )(tok, tok_row, cnt, hidden_in, grad_out, norm_gain[None], router_weight[None], gate_weight, up_weight, down_weight)
+    return grad_in, grad_gate, grad_up, grad_down, grad_gain[0], grad_router[0]
 
 
 def solution(mesh):

time: 473 us -> 150 us (0.32)
  blocking collectives: 255 us -> 0 us
  waiting for transfers between devices: 72.4 us -> 0 us
  Pallas kernels: 94 us -> 136 us
  matrix products: 22.8 us -> 0 us
  other arithmetic: 8.92 us -> 0 us
  starting transfers between devices: 8.33 us -> 0 us
    psum x2 -> x0, blocking collectives: 255 us -> none  [the longest x1 246 us: body(): lax.psum(jnp.concatenate([jnp.sum(d_normed * scaled, axis=0), router_part...]
    all_to_all x1 -> x0, waiting for transfers between devices: 72.4 us -> none  [body(): lax.all_to_all(parts, 'seq', 0, 0, tiled=True).astype(F32).sum(axis=0)]
    pallas_call x1, Pallas kernels: 94 us -> 136 us  [body(): pl.pallas_call(functools.partial(kernel, sizes), out_shape=(jax.ShapeDtyp...]
    dot_general x6 -> x0, matrix products: 22.8 us -> none  [the longest x1 4.29 us: body(): grad_down = jnp.einsum('pf,pd->fd', weighted, u, preferred_element_type=F32)]
    unnamed x22 -> x14, local copies, waits for them, and re-layouts: 0.04 us -> 9.03 us
    all_to_all x1 -> x0, starting transfers between devices: 8.33 us -> none  [body(): lax.all_to_all(parts, 'seq', 0, 0, tiled=True).astype(F32).sum(axis=0)]
    slice x2 -> x0, local copies, waits for them, and re-layouts: 4.86 us -> none  [the longest x1 4.75 us: body(): u = U[..., :cols].reshape(slots, cols)]
  transfers between devices with their start and end apart: 1 -> 0, of which waited for: 1 -> 0; matrix products, arithmetic and copies ran while one was open for 5% -> 0% of each run, Pallas kernels for 0% -> 0%
where the time goes in v2:
time: 150 us
  Pallas kernels  136 us (91%)
  local copies, waits for them, and re-layouts  12.2 us (8%)
    pallas_call x1, Pallas kernels, body(): pl.pallas_call(functools.partial(kernel, sizes), out_shape=(jax.ShapeDtyp...  136 us
    unnamed x14, local copies, waits for them, and re-layouts  9.03 us

profile of v2, /device:TPU:2, one launch (start us, length us, event | category | flops | bytes accessed | tf_op | source)
XLA Modules:
  0.0 149.9 jit_solution(7739389658375658856)
XLA Ops:
  1.3 0.6 broadcast_in_dim.29.cnt
  1.9 1.3 broadcast_in_dim.12.tok
  3.2 1.3 broadcast_in_dim.13.tok_row
  4.5 136.4 %block.1 = (bf16[128,2048]{1,0:T(8,128)(2,1)}, bf16[2048,384]{1,0:T(8,128)(2,1)}, bf16[2048,384]{1,0:T(8,128)(2,1)}, bf16[384,2048]{1,0:T(8,128)(2,1)}, f32[1,2048]{1,0:T(1,128)}, /*index=5*/f32[1,2048]{1,0:T(1,128)}) custom-call(s32[16,128]{1,0:T(8,128)} %broadcast_in_dim.12.tok, s32[128,16]{1,0:T(8,128)} %broadcast_in_dim.13.tok_row, ...), custom_call_target="tpu_custom_call" | custom-call | tf_op jit(solution)/shard_map/block/pallas_call | solution.py:470
  140.9 1.9 %copy.22 = bf16[128,2048]{1,0:T(8,128)(2,1)} copy(bf16[128,2048]{1,0:T(8,128)(2,1)} %get-tuple-element.24) | data formatting | bytes 1048576
  142.8 0.0 copy-start.1
  142.8 2.8 %copy.23 = bf16[2048,384]{1,0:T(8,128)(2,1)} copy(bf16[2048,384]{1,0:T(8,128)(2,1)} %get-tuple-element.25) | data formatting | bytes 3145728
  145.6 0.0 copy-done.1
  145.6 0.0 copy-start
  145.6 1.1 copy.24
  146.7 0.8 copy-done
  147.6 0.0 copy-start.3
  147.6 0.0 copy-start.2
  147.6 1.1 copy.25
  148.7 0.0 copy-done.3
  148.7 0.6 copy.26
  149.3 0.0 copy-done.2
  149.3 0.6 copy.27
Async XLA Ops:
  142.8 2.8 %copy-start.1 = (bf16[2048,384]{1,0:T(8,128)(2,1)S(1)}, bf16[2048,384]{1,0:T(8,128)(2,1)}, u32[]{:S(2)}) copy-start(bf16[2048,384]{1,0:T(8,128)(2,1)} %get-tuple-element.26) | copy-start | bytes 4718596
  145.6 2.0 %copy-start = (bf16[384,2048]{1,0:T(8,128)(2,1)S(1)}, bf16[384,2048]{1,0:T(8,128)(2,1)}, u32[]{:S(2)}) copy-start(bf16[384,2048]{1,0:T(8,128)(2,1)} %get-tuple-element.27) | copy-start | bytes 4718596
  147.6 1.1 copy-start.3
  147.6 1.7 %copy-start.2 = (f32[1,2048]{1,0:T(1,128)S(1)}, f32[1,2048]{1,0:T(1,128)}, u32[]{:S(2)}) copy-start(f32[1,2048]{1,0:T(1,128)} %get-tuple-element.17) | copy-start | bytes 24580

commit v3 on v1

v3 whole, which is shorter than its diff:
```python
import functools

import jax
import jax.numpy as jnp
from jax import lax
from jax.experimental import pallas as pl
from jax.experimental.pallas import tpu as pltpu
from jax.sharding import PartitionSpec as P

MESH = pl.DeviceIdType.MESH
BF = jnp.bfloat16
F32 = jnp.float32
norm_eps = 1e-06
NC = 2
CAP = 16
AUX = 128
TOK = 128
TILE = 256


def geometry(ny, nz, nx):
    s, t = lax.axis_index("seq"), lax.axis_index("tensor")
    c = lax.rem(s, NC)
    z = lax.rem(s // NC, nz)
    y = s // (NC * nz)
    way = 1 - 2 * c
    return y, z, c, t, way


def around(value, size):
    return lax.rem(value + 8 * size, size)


def step_of(k, way):
    far = (k + 1) // 2
    sign = (2 * lax.rem(k, 2) - 1) * way
    return sign, sign * far


def pair(value):
    high = value.astype(BF)
    return high, (value - high.astype(F32)).astype(BF)


def lanes(rows, columns):
    lane = lax.broadcasted_iota(jnp.int32, (rows, AUX), 1)
    total = jnp.zeros((rows, AUX), F32)
    for k, column in enumerate(columns):
        total = jnp.where(lane == k, jnp.broadcast_to(column, (rows, AUX)), total)
    return total


def dot(a, b, contract):
    return lax.dot_general(a, b, ((contract[0:1], contract[1:2]), ((), ())), preferred_element_type=F32)


def kernel(
    sizes,
    tok_hbm, cnt_hbm, hid_hbm, gro_hbm, gain_hbm, rw_hbm, wg_hbm, wu_hbm, wd_hbm,
    grad_in, grad_gate, grad_up, grad_down, grad_gain, grad_router,
    N, U, G, scaled_at, inv_at,
    sq, sb, rb_a, rb_b, rb_s,
    part, acc, y_far, y_near, z_in, v_acc, v_own, v_core, v_y, v_z,
    sem_sq, sem_nz, sem_ny, sem_uz, sem_uy, sem_dn, sem_du,
    sem_a, sem_b, sem_s, sem_g1, sem_g2, sem_gs,
    sem_t, sem_y, sem_z, sem_v, sem_vy, sem_vz, sent,
    tok, cnt, hid, gro, gain, rw, wg, wu, wd, sem_in,
):
    ny, nz, nx, width = sizes
    y, z, c, t, way = geometry(ny, nz, nx)
    cols = hid.shape[1]
    ff = wg.shape[1]
    rows = NC * CAP
    lag = 9

    def dev(yy, zz, cc, tt):
        return ((yy * nz + zz) * NC + cc, tt)

    def copy(src, dst, send, recv, to):
        return pltpu.make_async_remote_copy(
            src_ref=src, dst_ref=dst, send_sem=sent.at[send], recv_sem=recv, device_id=to, device_id_type=MESH
        )

    def same(ref, send, recv, to):
        return copy(ref, ref, send, recv, to)

    partner = dev(y, z, 1 - c, t)
    y_to = lambda d: dev(around(y + d, ny), z, c, t)
    z_to = lambda d: dev(y, around(z + d, nz), c, t)
    x_to = lambda d: dev(y, z, c, around(t + d, nx))

    loads = [
        pltpu.make_async_copy(far, near, sem_in.at[q])
        for q, (far, near) in enumerate((
            (tok_hbm, tok), (cnt_hbm, cnt), (hid_hbm, hid), (gain_hbm, gain), (rw_hbm, rw), (gro_hbm, gro),
            (wg_hbm, wg), (wu_hbm, wu), (wd_hbm, wd),
        ))
    ]
    for load in loads:
        load.start()
    barrier = pltpu.get_barrier_semaphore()
    peers = [y_to(d) for d in range(1, ny)] + [z_to(d) for d in range(1, nz)] + [x_to(d) for d in range(1, nx)] + [partner]
    for to in peers:
        pl.semaphore_signal(barrier, inc=1, device_id=to, device_id_type=MESH)

    def spread():
        return (lax.broadcasted_iota(jnp.int32, (TOK, CAP), 0) == tok[...]).astype(F32).astype(BF)

    for load in loads[0:5]:
        load.wait()
    live = lax.broadcasted_iota(jnp.int32, (CAP, 1), 0) < cnt[...]
    wide = dot(spread(), hid[...], (0, 0))
    rounded = rw[...].astype(BF).astype(F32)
    s1 = jnp.sum(wide * wide, axis=1, keepdims=True)
    s2 = jnp.sum(wide * (gain[...] * rounded), axis=1, keepdims=True)
    sq[t] = lanes(CAP, (s1, s2))

    pl.semaphore_wait(barrier, len(peers))
    for d in range(1, nx):
        same(sq.at[t], 0, sem_sq.at[t], x_to(d)).start()
    loads[5].wait()
    ups = dot(spread(), gro[...], (0, 0))
    U[z, y, c, :, 0:cols] = jnp.where(live, ups, 0.0).astype(BF)
    v_acc[...] = jnp.zeros_like(v_acc)
    for d in range(1, nx):
        frm = around(t + d, nx)
        same(sq.at[frm], 0, sem_sq.at[frm], x_to(d)).wait_recv()
    total = sq[0]
    for k in range(1, nx):
        total = total + sq[k]
    inverse = lax.rsqrt(total[:, 0:1] / width + norm_eps)
    scaled = wide * inverse
    N[z, y, c] = (scaled * gain[...]).astype(BF)
    scaled_at[...] = scaled
    inv_at[...] = jnp.broadcast_to(inverse, (CAP, AUX))
    high, low = pair(total[:, 1:2] * inverse)
    count = jnp.broadcast_to(cnt[...], (CAP, 1)).astype(F32)
    U[z, y, c, :, cols:] = lanes(CAP, (high.astype(F32), low.astype(F32), count)).astype(BF)

    def n_copy(zz, yy, send, recv, to):
        return same(N.at[zz, yy, c], send, recv, to)

    def u_copy(zz, yy, send, recv, to):
        return same(U.at[zz, yy, c], send, recv, to)

    def n_z_sends(yy):
        n_copy(z, yy, 2, sem_nz.at[1, yy], z_to(way)).start()
        if nz > 2:
            n_copy(z, yy, 2, sem_nz.at[2, yy], z_to(-way)).start()

    def u_y_sends(zz):
        u_copy(zz, y, 4, sem_uy.at[1, zz], y_to(way)).start()
        if ny > 2:
            u_copy(zz, y, 4, sem_uy.at[2, zz], y_to(-way)).start()

    def chunk_z(k):
        return around(z - step_of(k, way)[1], nz)

    def n_y_arrival(m):
        sign, far = step_of(m, way)
        yy = around(y - far, ny)
        n_copy(z, yy, 1, sem_ny.at[m], y_to(sign)).wait_recv()
        if m + 2 < ny:
            n_copy(z, yy, 1, sem_ny.at[m + 2], y_to(sign)).start()
        n_z_sends(yy)

    def u_y_arrival(k, m):
        zz = chunk_z(k)
        sign, far = step_of(m, way)
        yy = around(y - far, ny)
        u_copy(zz, yy, 4, sem_uy.at[m, zz], y_to(sign)).wait_recv()
        if m + 2 < ny:
            u_copy(zz, yy, 4, sem_uy.at[m + 2, zz], y_to(sign)).start()

    n_copy(z, y, 1, sem_ny.at[1], y_to(way)).start()
    if ny > 2:
        n_copy(z, y, 1, sem_ny.at[2], y_to(-way)).start()
    u_copy(z, y, 3, sem_uz.at[1], z_to(way)).start()
    if nz > 2:
        u_copy(z, y, 3, sem_uz.at[2], z_to(-way)).start()
    u_y_sends(z)
    n_z_sends(y)
    for m in range(1, ny):
        n_y_arrival(m)
        u_y_arrival(0, m)
    same(N.at[z, :, c], 5, sem_dn.at[z], partner).start()
    same(U.at[z, :, c], 6, sem_du.at[z], partner).start()

    def within(k, low, high):
        return pl.when((k >= low) & (k < high))

    def upstream_along_z(k):
        @within(k, 1, nz)
        def _():
            sign, far = step_of(k, way)
            zz = around(z - far, nz)
            u_copy(zz, y, 3, sem_uz.at[k], z_to(sign)).wait_recv()

            @pl.when(k + 2 < nz)
            def _():
                u_copy(zz, y, 3, sem_uz.at[k + 2], z_to(sign)).start()

            u_y_sends(zz)

    def upstream_along_y(k):
        @within(k, 1, nz)
        def _():
            for m in range(1, min(ny, 3)):
                u_y_arrival(k, m)

    def upstream_last(k):
        @within(k, 1, nz)
        def _():
            for m in range(3, ny):
                u_y_arrival(k, m)
            zz = chunk_z(k)
            same(U.at[zz, :, c], 6, sem_du.at[zz], partner).start()

    def normed_along_z(k):
        @within(k, 1, nz)
        def _():
            sign, far = step_of(k, way)
            zz = around(z - far, nz)
            for yy in range(ny):
                n_copy(zz, yy, 2, sem_nz.at[k, yy], z_to(sign)).wait_recv()

                @pl.when(k + 2 < nz)
                def _():
                    n_copy(zz, yy, 2, sem_nz.at[k + 2, yy], z_to(sign)).start()

            same(N.at[zz, :, c], 5, sem_dn.at[zz], partner).start()

    def x_block(i, d):
        return sb.at[i, around(t + d, nx)]

    def project(i):
        @within(i, 0, nz)
        def _():
            zz = chunk_z(i)
            same(N.at[zz, :, 1 - c], 5, sem_dn.at[zz], partner).wait_recv()
            same(U.at[zz, :, 1 - c], 6, sem_du.at[zz], partner).wait_recv()
            n = N[zz].reshape(ny * rows, cols)
            u = U[zz, :, :, :, 0:cols].reshape(ny * rows, cols)
            for q, out in enumerate((dot(n, wg[...], (1, 0)), dot(n, wu[...], (1, 0)), dot(u, wd[...], (1, 1)))):
                sb[i, :, :, q * ff:(q + 1) * ff] = out.astype(BF).reshape(nx, rows, ff)
            copy(x_block(i, 2), rb_a.at[i], 7, sem_a.at[i], x_to(way)).start()
            copy(x_block(i, -way), rb_s.at[i], 7, sem_s.at[i], x_to(-way)).start()

    def add(ref, other):
        ref[...] = (ref[...].astype(F32) + other[...].astype(F32)).astype(BF)

    def relay_sum(i):
        @within(i, 0, nz)
        def _():
            block = x_block(i, way)
            copy(block, rb_a.at[i], 7, sem_a.at[i], x_to(way)).wait_recv()
            add(block, rb_a.at[i])
            copy(block, rb_b.at[i], 7, sem_b.at[i], x_to(way)).start()

    def gate_backward(i):
        @within(i, 0, nz)
        def _():
            zz = chunk_z(i)
            block = x_block(i, 0)
            copy(block, rb_b.at[i], 7, sem_b.at[i], x_to(way)).wait_recv()
            copy(block, rb_s.at[i], 7, sem_s.at[i], x_to(-way)).wait_recv()
            full = sb[i, t].astype(F32) + rb_b[i].astype(F32) + rb_s[i].astype(F32)
            gate, upper, back = full[:, 0:ff], full[:, ff:2 * ff], full[:, 2 * ff:]
            aux = U[zz, t, :, :, cols:].reshape(rows, AUX).astype(F32)
            logits = aux[:, 0:1] + aux[:, 1:2]
            sig = jax.nn.sigmoid(gate)
            act = gate * sig
            slope = sig * (1.0 + gate * (1.0 - sig))
            hidden = act * upper
            d_hidden = logits * back
            d_gate = (d_hidden * upper * slope).astype(BF)
            d_up = (d_hidden * act).astype(BF)
            router = jnp.sum(hidden * back, axis=1, keepdims=True)
            inner = jnp.sum(d_gate.astype(F32) * gate + d_up.astype(F32) * upper, axis=1, keepdims=True) + router * logits
            G[zz, t, :, 0:ff] = d_gate
            G[zz, t, :, ff:2 * ff] = d_up
            G[zz, t, :, 2 * ff:3 * ff] = (hidden * logits).astype(BF)
            halves = pair(router) + pair(inner)
            G[zz, t, :, 3 * ff:] = lanes(rows, [v.astype(F32) for v in halves]).astype(BF)
            same(G.at[zz, t], 8, sem_g1.at[i], x_to(way)).start()
            same(G.at[zz, t], 8, sem_gs.at[i], x_to(-way)).start()

    def relay_gradients(i):
        @within(i, 0, nz)
        def _():
            block = G.at[chunk_z(i), around(t - way, nx)]
            same(block, 8, sem_g1.at[i], x_to(way)).wait_recv()
            same(block, 8, sem_g2.at[i], x_to(way)).start()

    def rows_backward(i):
        @within(i, 0, nz)
        def _():
            zz = chunk_z(i)
            same(G.at[zz, around(t + way, nx)], 8, sem_gs.at[i], x_to(-way)).wait_recv()
            same(G.at[zz, around(t + 2, nx)], 8, sem_g2.at[i], x_to(way)).wait_recv()
            g = G[zz].reshape(ny * rows, 3 * ff + AUX)
            out = dot(g[:, 0:ff], wg[...], (1, 1)) + dot(g[:, ff:2 * ff], wu[...], (1, 1))
            part[zz, :, :, :, 0:cols] = out.astype(BF).reshape(ny, NC, CAP, cols)
            part[zz, :, :, :, cols:] = g[:, 3 * ff:].reshape(ny, NC, CAP, AUX)
            copy(part.at[zz, :, 1 - c], acc.at[zz], 9, sem_t.at[zz], partner).start()
            n = N[zz].reshape(ny * rows, cols).astype(F32)
            aux = g[:, 3 * ff:].astype(F32)
            router = aux[:, 0:1] + aux[:, 1:2]
            v_acc[0] += jnp.sum((out * n).reshape(-1, 8, cols), axis=0)
            v_acc[1] += jnp.sum((n * router).reshape(-1, 8, cols), axis=0)

    def y_start(i):
        @within(i, 0, nz)
        def _():
            zz = chunk_z(i)
            copy(part.at[zz, :, 1 - c], acc.at[zz], 9, sem_t.at[zz], partner).wait_recv()
            acc[zz] = (acc[zz].astype(F32) + part[zz, :, c].astype(F32)).astype(BF)
            copy(acc.at[zz, around(y + 2, ny)], y_far.at[zz, 1], 10, sem_y.at[zz, 1], y_to(way)).start()
            copy(acc.at[zz, around(y - way, ny)], y_near.at[zz], 10, sem_y.at[zz, 2], y_to(-way)).start()

    def y_relay(i):
        @within(i, 0, nz)
        def _():
            zz = chunk_z(i)
            block = acc.at[zz, around(y + way, ny)]
            copy(block, y_far.at[zz, 1], 10, sem_y.at[zz, 1], y_to(way)).wait_recv()
            add(block, y_far.at[zz, 1])
            copy(block, y_far.at[zz, 0], 10, sem_y.at[zz, 0], y_to(way)).start()

    def y_end(i):
        @within(i, 0, nz)
        def _():
            zz = chunk_z(i)
            block = acc.at[zz, y]
            copy(block, y_near.at[zz], 10, sem_y.at[zz, 2], y_to(-way)).wait_recv()
            copy(block, y_far.at[zz, 0], 10, sem_y.at[zz, 0], y_to(way)).wait_recv()
            total = block[...].astype(F32) + y_near[zz].astype(F32) + y_far[zz, 0].astype(F32)
            block[...] = total.astype(BF)

            @pl.when(i > 0)
            def _():
                copy(block, z_in.at[z], 11, sem_z.at[z], dev(y, zz, c, t)).start()

            @pl.when(i == 0)
            def _():
                z_in[z] = block[...]

    own_sums = copy(v_own, v_core, 12, sem_v.at[0], partner)

    def sums_start():
        v_own[...] = jnp.sum(v_acc[...], axis=1)
        own_sums.start()

    def sums_y():
        own_sums.wait_recv()
        v_y[y] = v_own[...] + v_core[...]
        for d in range(1, ny):
            same(v_y.at[y], 13, sem_vy.at[y], y_to(d)).start()

    def sums_z():
        for d in range(1, ny):
            frm = around(y + d, ny)
            same(v_y.at[frm], 13, sem_vy.at[frm], y_to(d)).wait_recv()
        total = v_y[0]
        for k in range(1, ny):
            total = total + v_y[k]
        v_z[z] = total
        for d in range(1, nz):
            same(v_z.at[z], 14, sem_vz.at[z], z_to(d)).start()

    def scale():
        counts = U[:, :, :, :, cols:].reshape(-1, AUX).astype(F32)
        return lax.rsqrt(jnp.sum(counts, axis=0, keepdims=True)[:, 2:3] / CAP)

    def tile(i, carry):
        columns = pl.ds(pl.multiple_of(i * TILE, TILE), TILE)
        slots = ny * nz * rows
        n = N[:, :, :, :, columns].reshape(slots, TILE)
        u = U[:, :, :, :, columns].reshape(slots, TILE)
        g = G[:, :, :, 0:3 * ff].reshape(slots, 3 * ff)
        count_scale = scale()
        both = (dot(n, g[:, 0:2 * ff], (0, 0)) * count_scale).astype(BF)
        grad_gate[columns] = both[:, 0:ff]
        grad_up[columns] = both[:, ff:]
        grad_down[:, columns] = (dot(g[:, 2 * ff:], u, (0, 0)) * count_scale).astype(BF)
        return carry

    for load in loads[6:9]:
        load.wait()
    tiles = cols // TILE
    last = nz - 1 + lag
    each = max(tiles // 4, 1)

    def loop(k, carry):
        upstream_along_z(2 * k - 1)
        upstream_along_z(2 * k)
        upstream_along_y(2 * k - 3)
        upstream_along_y(2 * k - 2)
        upstream_last(2 * k - 5)
        upstream_last(2 * k - 4)
        normed_along_z(k)
        rows_backward(k - 6)
        relay_gradients(k - 5)
        gate_backward(k - 4)
        y_end(k - 9)
        y_relay(k - 8)
        y_start(k - 7)
        relay_sum(k - 3)
        project(k - 2)
        pl.when(k == last - 3)(sums_start)
        pl.when(k == last - 2)(sums_y)
        pl.when(k == last - 1)(sums_z)
        begin = jnp.where(k >= last - 3, (k - (last - 3)) * each, 0)
        end = jnp.where(k >= last - 3, begin + each, 0)
        lax.fori_loop(begin, end, tile, 0)
        return carry

    lax.fori_loop(0, last + 1, loop, 0)

    for d in range(1, nz):
        frm = around(z + d, nz)
        same(v_z.at[frm], 14, sem_vz.at[frm], z_to(d)).wait_recv()
    sums = v_z[0]
    for k in range(1, nz):
        sums = sums + v_z[k]
    gain_sum, router_sum = sums[0:1], sums[1:2]
    count_scale = scale()
    grad_router[...] = count_scale * router_sum
    grad_gain[...] = count_scale * ((gain_sum + rw[...] * router_sum) / gain[...])

    for d in range(1, nz):
        frm = around(z + d, nz)
        copy(z_in.at[frm], z_in.at[frm], 11, sem_z.at[frm], z_to(d)).wait_recv()
    mine = z_in[0].astype(F32)
    for k in range(1, nz):
        mine = mine + z_in[k].astype(F32)
    router = mine[:, cols:cols + 1] + mine[:, cols + 1:cols + 2]
    inner = (mine[:, cols + 2:cols + 3] + mine[:, cols + 3:cols + 4]) / width
    d_normed = mine[:, 0:cols] + router * rw[...]
    d_picked = inv_at[:, 0:1] * (d_normed * gain[...] - scaled_at[...] * inner)
    high, low = pair(jnp.where(live, d_picked, 0.0))
    grad_in[...] = (gro[...].astype(F32) + dot(spread(), high, (1, 0)) + dot(spread(), low, (1, 0))).astype(BF)

    def drain(ref, send):
        same(ref, send, sem_sq.at[0], partner).wait_send()

    drain(sq.at[0:nx - 1], 0)
    drain(N.at[0, 0:ny - 1, 0], 1)
    drain(N.at[0:nz - 1, :, 0], 2)
    drain(U.at[0:nz - 1, 0, 0], 3)
    drain(U.at[:, 0:ny - 1, 0], 4)
    drain(N.at[:, :, 0], 5)
    drain(U.at[:, :, 0], 6)
    drain(sb.at[:, 0:3], 7)
    drain(G.at[:, 0:3], 8)
    drain(acc, 9)
    drain(acc.at[:, 0:3], 10)
    drain(z_in.at[0:nz - 1], 11)
    drain(v_own, 12)
    drain(v_y.at[0:ny - 1], 13)
    drain(v_z.at[0:nz - 1], 14)


def body(hidden_in, grad_out, slot_tokens, live_counts, norm_gain, router_weight, gate_weight, up_weight, down_weight, sizes):
    ny, nz, nx, width = sizes
    cols, ff = gate_weight.shape
    rows = NC * CAP
    vmem = pl.BlockSpec(memory_space=pltpu.VMEM)
    dma = pltpu.SemaphoreType.DMA
    scratch = pltpu.VMEM
    grad_in, grad_gate, grad_up, grad_down, grad_gain, grad_router = pl.pallas_call(
        functools.partial(kernel, sizes),
        out_shape=(
            scratch(grad_out.shape, BF),
            scratch((cols, ff), BF),
            scratch((cols, ff), BF),
            scratch((ff, cols), BF),
            scratch((1, cols), F32),
            scratch((1, cols), F32),
        ),
        in_specs=[pl.BlockSpec(memory_space=pltpu.HBM)] * 9,
        out_specs=[vmem] * 6,
        scratch_shapes=[
            scratch((nz, ny, NC, CAP, cols), BF),
            scratch((nz, ny, NC, CAP, cols + AUX), BF),
            scratch((nz, nx, rows, 3 * ff + AUX), BF),
            scratch((CAP, cols), F32),
            scratch((CAP, AUX), F32),
            scratch((nx, CAP, AUX), F32),
            scratch((nz, nx, rows, 3 * ff), BF),
            scratch((nz, rows, 3 * ff), BF),
            scratch((nz, rows, 3 * ff), BF),
            scratch((nz, rows, 3 * ff), BF),
            scratch((nz, ny, NC, CAP, cols + AUX), BF),
            scratch((nz, ny, CAP, cols + AUX), BF),
            scratch((nz, 2, CAP, cols + AUX), BF),
            scratch((nz, CAP, cols + AUX), BF),
            scratch((nz, CAP, cols + AUX), BF),
            scratch((2, 8, cols), F32),
            scratch((2, cols), F32),
            scratch((2, cols), F32),
            scratch((ny, 2, cols), F32),
            scratch((nz, 2, cols), F32),
            dma((nx,)), dma((nz, ny)), dma((ny,)), dma((nz,)), dma((ny, nz)), dma((nz,)), dma((nz,)),
            dma((nz,)), dma((nz,)), dma((nz,)), dma((nz,)), dma((nz,)), dma((nz,)),
            dma((nz,)), dma((nz, 3)), dma((nz,)), dma((1,)), dma((ny,)), dma((nz,)), dma((15,)),
            scratch((1, CAP), jnp.int32), scratch((1, 1), jnp.int32),
            scratch(hidden_in.shape, BF), scratch(grad_out.shape, BF), scratch((1, cols), F32), scratch((1, cols), F32),
            scratch((cols, ff), BF), scratch((cols, ff), BF), scratch((ff, cols), BF), dma((9,)),
        ],
        compiler_params=pltpu.CompilerParams(collective_id=0, has_side_effects=True, vmem_limit_bytes=60000000),
        name="block",
    )(
        slot_tokens[None], live_counts[None], hidden_in, grad_out, norm_gain[None], router_weight[None],
        gate_weight, up_weight, down_weight,
    )
    return grad_in, grad_gate, grad_up, grad_down, grad_gain[0], grad_router[0]


def solution(mesh):
    nx = mesh.shape["tensor"]
    ny = nx
    nz = mesh.shape["seq"] // (ny * NC)
    weights = (P("tensor", "seq"), P("tensor", "seq"), P("seq", "tensor"))
    in_specs = (P("seq", "tensor"), P("seq", "tensor"), P("seq"), P("seq"), P("tensor"), P("tensor")) + weights
    out_specs = (P("seq", "tensor"),) + weights + (P("tensor"), P("tensor"))

    def whole(hidden_in, *rest):
        sizes = (ny, nz, nx, hidden_in.shape[1] * nx)
        return body(hidden_in, *rest, sizes)

    return jax.shard_map(whole, mesh=mesh, in_specs=in_specs, out_specs=out_specs, check_vma=False)
```

time: 473 us -> 115 us (0.24)
  blocking collectives: 255 us -> 0 us
  waiting for transfers between devices: 72.4 us -> 0 us
  matrix products: 22.8 us -> 0 us
  Pallas kernels: 94 us -> 107 us
  other arithmetic: 8.92 us -> 0 us
  starting transfers between devices: 8.33 us -> 0 us
    psum x2 -> x0, blocking collectives: 255 us -> none  [the longest x1 246 us: body(): lax.psum(jnp.concatenate([jnp.sum(d_normed * scaled, axis=0), router_part...]
    all_to_all x1 -> x0, waiting for transfers between devices: 72.4 us -> none  [body(): lax.all_to_all(parts, 'seq', 0, 0, tiled=True).astype(F32).sum(axis=0)]
    dot_general x6 -> x0, matrix products: 22.8 us -> none  [the longest x1 4.29 us: body(): grad_down = jnp.einsum('pf,pd->fd', weighted, u, preferred_element_type=F32)]
    pallas_call x1, Pallas kernels: 94 us -> 107 us  [body(): pl.pallas_call(functools.partial(kernel, sizes), out_shape=(scratch(grad_...]
    all_to_all x1 -> x0, starting transfers between devices: 8.33 us -> none  [body(): lax.all_to_all(parts, 'seq', 0, 0, tiled=True).astype(F32).sum(axis=0)]
    unnamed x22 -> x6, local copies, waits for them, and re-layouts: 0.04 us -> 5.42 us
    slice x2 -> x0, local copies, waits for them, and re-layouts: 4.86 us -> none  [the longest x1 4.75 us: body(): u = U[..., :cols].reshape(slots, cols)]
  transfers between devices with their start and end apart: 1 -> 0, of which waited for: 1 -> 0; matrix products, arithmetic and copies ran while one was open for 5% -> 0% of each run, Pallas kernels for 0% -> 0%
where the time goes in v3:
time: 115 us; the launch traced here: 114 us
  Pallas kernels  107 us (93%)
  local copies, waits for them, and re-layouts  5.42 us (5%)
  between operations  1.29 us (1%)
    pallas_call x1, Pallas kernels, body(): pl.pallas_call(functools.partial(kernel, sizes), out_shape=(scratch(grad_...  107 us
    unnamed x6, local copies, waits for them, and re-layouts  5.42 us

profile of v3, /device:TPU:2, one launch (start us, length us, event | category | flops | bytes accessed | tf_op | source)
XLA Modules:
  0.0 113.9 jit_solution(18311950457178111063)
XLA Ops:
  1.3 107.2 %block.1 = (bf16[128,2048]{1,0:T(8,128)(2,1)S(1)}, bf16[2048,384]{1,0:T(8,128)(2,1)S(1)}, bf16[2048,384]{1,0:T(8,128)(2,1)S(1)}, bf16[384,2048]{1,0:T(8,128)(2,1...) custom-call(s32[1,16]{1,0:T(1,128)} %bitcast.11, s32[1,1]{1,0:T(1,128)} %bitcast.6.cnt_hbm, ...), custom_call_target="tpu_custom_call" | custom-call | tf_op jit(solution)/shard_map/block/pallas_call | solution.py:471
  108.5 0.8 copy.21
  109.3 0.6 copy.25
  109.9 0.6 copy.26
  110.5 1.1 %copy.22 = bf16[2048,384]{1,0:T(8,128)(2,1)} copy(bf16[2048,384]{1,0:T(8,128)(2,1)S(1)} %get-tuple-element.19) | data formatting | bytes 3145728
  111.6 1.1 %copy.23 = bf16[2048,384]{1,0:T(8,128)(2,1)} copy(bf16[2048,384]{1,0:T(8,128)(2,1)S(1)} %get-tuple-element.20) | data formatting | bytes 3145728
  112.8 1.1 %copy.24 = bf16[384,2048]{1,0:T(8,128)(2,1)} copy(bf16[384,2048]{1,0:T(8,128)(2,1)S(1)} %get-tuple-element.21) | data formatting | bytes 3145728

commit v4 on v3

--- a/solution.py
+++ b/solution.py
@@ -58,9 +58,9 @@
     sizes,
     tok_hbm, cnt_hbm, hid_hbm, gro_hbm, gain_hbm, rw_hbm, wg_hbm, wu_hbm, wd_hbm,
     grad_in, grad_gate, grad_up, grad_down, grad_gain, grad_router,
-    N, U, G, scaled_at, inv_at,
+    N, NN, U, G, scaled_at, inv_at,
     sq, sb, rb_a, rb_b, rb_s,
-    part, acc, y_far, y_near, z_in, v_acc, v_own, v_core, v_y, v_z,
+    part, acc, y_in, z_in, v_acc, v_own, v_core, v_y, v_z,
     sem_sq, sem_nz, sem_ny, sem_uz, sem_uy, sem_dn, sem_du,
     sem_a, sem_b, sem_s, sem_g1, sem_g2, sem_gs,
     sem_t, sem_y, sem_z, sem_v, sem_vy, sem_vz, sent,
@@ -71,7 +71,7 @@
     cols = hid.shape[1]
     ff = wg.shape[1]
     rows = NC * CAP
-    lag = 9
+    lag = 7
 
     def dev(yy, zz, cc, tt):
         return ((yy * nz + zz) * NC + cc, tt)
@@ -114,10 +114,50 @@
     s1 = jnp.sum(wide * wide, axis=1, keepdims=True)
     s2 = jnp.sum(wide * (gain[...] * rounded), axis=1, keepdims=True)
     sq[t] = lanes(CAP, (s1, s2))
+    N[z, y, c] = wide.astype(BF)
+
+    def n_copy(zz, yy, send, recv, to):
+        return same(N.at[zz, yy, c], send, recv, to)
+
+    def u_copy(zz, yy, send, recv, to):
+        return same(U.at[zz, yy, c], send, recv, to)
+
+    def n_z_sends(yy):
+        n_copy(z, yy, 2, sem_nz.at[1, yy], z_to(way)).start()
+        if nz > 2:
+            n_copy(z, yy, 2, sem_nz.at[2, yy], z_to(-way)).start()
+
+    def u_y_sends(zz):
+        u_copy(zz, y, 4, sem_uy.at[1, zz], y_to(way)).start()
+        if ny > 2:
+            u_copy(zz, y, 4, sem_uy.at[2, zz], y_to(-way)).start()
+
+    def chunk_z(k):
+        return around(z - step_of(k, way)[1], nz)
+
+    def n_y_arrival(m):
+        sign, far = step_of(m, way)
+        yy = around(y - far, ny)
+        n_copy(z, yy, 1, sem_ny.at[m], y_to(sign)).wait_recv()
+        if m + 2 < ny:
+            n_copy(z, yy, 1, sem_ny.at[m + 2], y_to(sign)).start()
+        n_z_sends(yy)
+
+    def u_y_arrival(k, m):
+        zz = chunk_z(k)
+        sign, far = step_of(m, way)
+        yy = around(y - far, ny)
+        u_copy(zz, yy, 4, sem_uy.at[m, zz], y_to(sign)).wait_recv()
+        if m + 2 < ny:
+            u_copy(zz, yy, 4, sem_uy.at[m + 2, zz], y_to(sign)).start()
 
     pl.semaphore_wait(barrier, len(peers))
+    n_copy(z, y, 1, sem_ny.at[1], y_to(way)).start()
+    if ny > 2:
+        n_copy(z, y, 1, sem_ny.at[2], y_to(-way)).start()
     for d in range(1, nx):
         same(sq.at[t], 0, sem_sq.at[t], x_to(d)).start()
+    n_z_sends(y)
     loads[5].wait()
     ups = dot(spread(), gro[...], (0, 0))
     U[z, y, c, :, 0:cols] = jnp.where(live, ups, 0.0).astype(BF)
@@ -129,62 +169,23 @@
     for k in range(1, nx):
         total = total + sq[k]
     inverse = lax.rsqrt(total[:, 0:1] / width + norm_eps)
-    scaled = wide * inverse
-    N[z, y, c] = (scaled * gain[...]).astype(BF)
-    scaled_at[...] = scaled
+    scaled_at[...] = wide * inverse
     inv_at[...] = jnp.broadcast_to(inverse, (CAP, AUX))
-    high, low = pair(total[:, 1:2] * inverse)
     count = jnp.broadcast_to(cnt[...], (CAP, 1)).astype(F32)
-    U[z, y, c, :, cols:] = lanes(CAP, (high.astype(F32), low.astype(F32), count)).astype(BF)
-
-    def n_copy(zz, yy, send, recv, to):
-        return same(N.at[zz, yy, c], send, recv, to)
-
-    def u_copy(zz, yy, send, recv, to):
-        return same(U.at[zz, yy, c], send, recv, to)
-
-    def n_z_sends(yy):
-        n_copy(z, yy, 2, sem_nz.at[1, yy], z_to(way)).start()
-        if nz > 2:
-            n_copy(z, yy, 2, sem_nz.at[2, yy], z_to(-way)).start()
-
-    def u_y_sends(zz):
-        u_copy(zz, y, 4, sem_uy.at[1, zz], y_to(way)).start()
-        if ny > 2:
-            u_copy(zz, y, 4, sem_uy.at[2, zz], y_to(-way)).start()
-
-    def chunk_z(k):
-        return around(z - step_of(k, way)[1], nz)
-
-    def n_y_arrival(m):
-        sign, far = step_of(m, way)
-        yy = around(y - far, ny)
-        n_copy(z, yy, 1, sem_ny.at[m], y_to(sign)).wait_recv()
-        if m + 2 < ny:
-            n_copy(z, yy, 1, sem_ny.at[m + 2], y_to(sign)).start()
-        n_z_sends(yy)
-
-    def u_y_arrival(k, m):
-        zz = chunk_z(k)
-        sign, far = step_of(m, way)
-        yy = around(y - far, ny)
-        u_copy(zz, yy, 4, sem_uy.at[m, zz], y_to(sign)).wait_recv()
-        if m + 2 < ny:
-            u_copy(zz, yy, 4, sem_uy.at[m + 2, zz], y_to(sign)).start()
-
-    n_copy(z, y, 1, sem_ny.at[1], y_to(way)).start()
-    if ny > 2:
-        n_copy(z, y, 1, sem_ny.at[2], y_to(-way)).start()
+    halves = [v.astype(F32) for v in pair(total[:, 1:2] * inverse) + pair(inverse)]
+    U[z, y, c, :, cols:] = lanes(CAP, halves[0:2] + [count] + halves[2:4]).astype(BF)
+    u_y_sends(z)
     u_copy(z, y, 3, sem_uz.at[1], z_to(way)).start()
     if nz > 2:
         u_copy(z, y, 3, sem_uz.at[2], z_to(-way)).start()
-    u_y_sends(z)
-    n_z_sends(y)
     for m in range(1, ny):
         n_y_arrival(m)
+    same(N.at[z, :, c], 5, sem_dn.at[z], partner).start()
+    for m in range(1, ny):
         u_y_arrival(0, m)
-    same(N.at[z, :, c], 5, sem_dn.at[z], partner).start()
     same(U.at[z, :, c], 6, sem_du.at[z], partner).start()
+    for load in loads[6:9]:
+        load.wait()
 
     def within(k, low, high):
         return pl.when((k >= low) & (k < high))
@@ -239,7 +240,10 @@
             zz = chunk_z(i)
             same(N.at[zz, :, 1 - c], 5, sem_dn.at[zz], partner).wait_recv()
             same(U.at[zz, :, 1 - c], 6, sem_du.at[zz], partner).wait_recv()
-            n = N[zz].reshape(ny * rows, cols)
+            aux = U[zz, :, :, :, cols:].reshape(ny * rows, AUX).astype(F32)
+            inverse = aux[:, 3:4] + aux[:, 4:5]
+            n = (N[zz].reshape(ny * rows, cols).astype(F32) * inverse * gain[...]).astype(BF)
+            NN[zz] = n.reshape(ny, NC, CAP, cols)
             u = U[zz, :, :, :, 0:cols].reshape(ny * rows, cols)
             for q, out in enumerate((dot(n, wg[...], (1, 0)), dot(n, wu[...], (1, 0)), dot(u, wd[...], (1, 1)))):
                 sb[i, :, :, q * ff:(q + 1) * ff] = out.astype(BF).reshape(nx, rows, ff)
@@ -303,7 +307,7 @@
             part[zz, :, :, :, 0:cols] = out.astype(BF).reshape(ny, NC, CAP, cols)
             part[zz, :, :, :, cols:] = g[:, 3 * ff:].reshape(ny, NC, CAP, AUX)
             copy(part.at[zz, :, 1 - c], acc.at[zz], 9, sem_t.at[zz], partner).start()
-            n = N[zz].reshape(ny * rows, cols).astype(F32)
+            n = NN[zz].reshape(ny * rows, cols).astype(F32)
             aux = g[:, 3 * ff:].astype(F32)
             router = aux[:, 0:1] + aux[:, 1:2]
             v_acc[0] += jnp.sum((out * n).reshape(-1, 8, cols), axis=0)
@@ -315,26 +319,20 @@
             zz = chunk_z(i)
             copy(part.at[zz, :, 1 - c], acc.at[zz], 9, sem_t.at[zz], partner).wait_recv()
             acc[zz] = (acc[zz].astype(F32) + part[zz, :, c].astype(F32)).astype(BF)
-            copy(acc.at[zz, around(y + 2, ny)], y_far.at[zz, 1], 10, sem_y.at[zz, 1], y_to(way)).start()
-            copy(acc.at[zz, around(y - way, ny)], y_near.at[zz], 10, sem_y.at[zz, 2], y_to(-way)).start()
-
-    def y_relay(i):
-        @within(i, 0, nz)
-        def _():
-            zz = chunk_z(i)
-            block = acc.at[zz, around(y + way, ny)]
-            copy(block, y_far.at[zz, 1], 10, sem_y.at[zz, 1], y_to(way)).wait_recv()
-            add(block, y_far.at[zz, 1])
-            copy(block, y_far.at[zz, 0], 10, sem_y.at[zz, 0], y_to(way)).start()
+            for d in range(1, ny):
+                yy = around(y + d, ny)
+                copy(acc.at[zz, yy], y_in.at[zz, d - 1], 10, sem_y.at[zz, d - 1], y_to(d)).start()
 
     def y_end(i):
         @within(i, 0, nz)
         def _():
             zz = chunk_z(i)
             block = acc.at[zz, y]
-            copy(block, y_near.at[zz], 10, sem_y.at[zz, 2], y_to(-way)).wait_recv()
-            copy(block, y_far.at[zz, 0], 10, sem_y.at[zz, 0], y_to(way)).wait_recv()
-            total = block[...].astype(F32) + y_near[zz].astype(F32) + y_far[zz, 0].astype(F32)
+            for d in range(1, ny):
+                copy(block, y_in.at[zz, d - 1], 10, sem_y.at[zz, d - 1], y_to(d)).wait_recv()
+            total = block[...].astype(F32)
+            for d in range(1, ny):
+                total = total + y_in[zz, d - 1].astype(F32)
             block[...] = total.astype(BF)
 
             @pl.when(i > 0)
@@ -375,7 +373,7 @@
     def tile(i, carry):
         columns = pl.ds(pl.multiple_of(i * TILE, TILE), TILE)
         slots = ny * nz * rows
-        n = N[:, :, :, :, columns].reshape(slots, TILE)
+        n = NN[:, :, :, :, columns].reshape(slots, TILE)
         u = U[:, :, :, :, columns].reshape(slots, TILE)
         g = G[:, :, :, 0:3 * ff].reshape(slots, 3 * ff)
         count_scale = scale()
@@ -385,33 +383,33 @@
         grad_down[:, columns] = (dot(g[:, 2 * ff:], u, (0, 0)) * count_scale).astype(BF)
         return carry
 
-    for load in loads[6:9]:
-        load.wait()
     tiles = cols // TILE
     last = nz - 1 + lag
-    each = max(tiles // 4, 1)
+    each = -(-tiles // 3)
+
+    def early(k, late):
+        return jnp.where(k == late - 1, 0, jnp.where(k == late, -1, k - late))
 
     def loop(k, carry):
-        upstream_along_z(2 * k - 1)
-        upstream_along_z(2 * k)
-        upstream_along_y(2 * k - 3)
-        upstream_along_y(2 * k - 2)
-        upstream_last(2 * k - 5)
-        upstream_last(2 * k - 4)
-        normed_along_z(k)
-        rows_backward(k - 6)
-        relay_gradients(k - 5)
-        gate_backward(k - 4)
-        y_end(k - 9)
-        y_relay(k - 8)
-        y_start(k - 7)
-        relay_sum(k - 3)
-        project(k - 2)
-        pl.when(k == last - 3)(sums_start)
-        pl.when(k == last - 2)(sums_y)
-        pl.when(k == last - 1)(sums_z)
-        begin = jnp.where(k >= last - 3, (k - (last - 3)) * each, 0)
-        end = jnp.where(k >= last - 3, begin + each, 0)
+        upstream_along_z(2 * k + 1)
+        upstream_along_z(2 * k + 2)
+        upstream_along_y(2 * k - 1)
+        upstream_along_y(2 * k)
+        upstream_last(2 * k - 3)
+        upstream_last(2 * k - 2)
+        normed_along_z(k + 1)
+        project(early(k, 1))
+        relay_sum(early(k, 2))
+        gate_backward(early(k, 3))
+        relay_gradients(early(k, 4))
+        rows_backward(early(k, 5))
+        y_start(early(k, 6))
+        y_end(early(k, 7))
+        pl.when(k == last - 2)(sums_start)
+        pl.when(k == last - 1)(sums_y)
+        pl.when(k == last)(sums_z)
+        begin = jnp.clip((k - (last - 2)) * each, 0, tiles)
+        end = jnp.clip((k - (last - 3)) * each, 0, tiles)
         lax.fori_loop(begin, end, tile, 0)
         return carry
 
@@ -454,7 +452,7 @@
     drain(sb.at[:, 0:3], 7)
     drain(G.at[:, 0:3], 8)
     drain(acc, 9)
-    drain(acc.at[:, 0:3], 10)
+    drain(acc.at[:, 0:ny - 1], 10)
     drain(z_in.at[0:nz - 1], 11)
     drain(v_own, 12)
     drain(v_y.at[0:ny - 1], 13)
@@ -482,6 +480,7 @@
         out_specs=[vmem] * 6,
         scratch_shapes=[
             scratch((nz, ny, NC, CAP, cols), BF),
+            scratch((nz, ny, NC, CAP, cols), BF),
             scratch((nz, ny, NC, CAP, cols + AUX), BF),
             scratch((nz, nx, rows, 3 * ff + AUX), BF),
             scratch((CAP, cols), F32),
@@ -493,8 +492,7 @@
             scratch((nz, rows, 3 * ff), BF),
             scratch((nz, ny, NC, CAP, cols + AUX), BF),
             scratch((nz, ny, CAP, cols + AUX), BF),
-            scratch((nz, 2, CAP, cols + AUX), BF),
-            scratch((nz, CAP, cols + AUX), BF),
+            scratch((nz, ny - 1, CAP, cols + AUX), BF),
             scratch((nz, CAP, cols + AUX), BF),
             scratch((2, 8, cols), F32),
             scratch((2, cols), F32),
@@ -503,7 +501,7 @@
             scratch((nz, 2, cols), F32),
             dma((nx,)), dma((nz, ny)), dma((ny,)), dma((nz,)), dma((ny, nz)), dma((nz,)), dma((nz,)),
             dma((nz,)), dma((nz,)), dma((nz,)), dma((nz,)), dma((nz,)), dma((nz,)),
-            dma((nz,)), dma((nz, 3)), dma((nz,)), dma((1,)), dma((ny,)), dma((nz,)), dma((15,)),
+            dma((nz,)), dma((nz, ny - 1)), dma((nz,)), dma((1,)), dma((ny,)), dma((nz,)), dma((15,)),
             scratch((1, CAP), jnp.int32), scratch((1, 1), jnp.int32),
             scratch(hidden_in.shape, BF), scratch(grad_out.shape, BF), scratch((1, cols), F32), scratch((1, cols), F32),
             scratch((cols, ff), BF), scratch((cols, ff), BF), scratch((ff, cols), BF), dma((9,)),

time: 115 us -> 114 us (level)
    pallas_call x1, Pallas kernels: 107 us -> 106 us  [body(): pl.pallas_call(functools.partial(kernel, sizes), out_shape=(scratch(grad_...]
where the time goes in v4:
time: 114 us; the launch traced here: 113 us
  Pallas kernels  106 us (93%)
  local copies, waits for them, and re-layouts  5.42 us (5%)
  between operations  1.29 us (1%)
    pallas_call x1, Pallas kernels, body(): pl.pallas_call(functools.partial(kernel, sizes), out_shape=(scratch(grad_...  106 us
    unnamed x6, local copies, waits for them, and re-layouts  5.42 us

profile of v4, /device:TPU:2, one launch (start us, length us, event | category | flops | bytes accessed | tf_op | source)
XLA Modules:
  0.0 112.5 jit_solution(7193359782236197359)
XLA Ops:
  1.3 105.8 %block.1 = (bf16[128,2048]{1,0:T(8,128)(2,1)S(1)}, bf16[2048,384]{1,0:T(8,128)(2,1)S(1)}, bf16[2048,384]{1,0:T(8,128)(2,1)S(1)}, bf16[384,2048]{1,0:T(8,128)(2,1...) custom-call(s32[1,16]{1,0:T(1,128)} %bitcast.11, s32[1,1]{1,0:T(1,128)} %bitcast.6.cnt_hbm, ...), custom_call_target="tpu_custom_call" | custom-call | tf_op jit(solution)/shard_map/block/pallas_call | solution.py:469
  107.1 0.8 copy.21
  107.9 0.6 copy.25
  108.5 0.6 copy.26
  109.1 1.1 %copy.22 = bf16[2048,384]{1,0:T(8,128)(2,1)} copy(bf16[2048,384]{1,0:T(8,128)(2,1)S(1)} %get-tuple-element.19) | data formatting | bytes 3145728
  110.3 1.1 %copy.23 = bf16[2048,384]{1,0:T(8,128)(2,1)} copy(bf16[2048,384]{1,0:T(8,128)(2,1)S(1)} %get-tuple-element.20) | data formatting | bytes 3145728
  111.4 1.1 %copy.24 = bf16[384,2048]{1,0:T(8,128)(2,1)} copy(bf16[384,2048]{1,0:T(8,128)(2,1)S(1)} %get-tuple-element.21) | data formatting | bytes 3145728

commit v5 on v4

--- a/solution.py
+++ b/solution.py
@@ -64,7 +64,7 @@
     sem_sq, sem_nz, sem_ny, sem_uz, sem_uy, sem_dn, sem_du,
     sem_a, sem_b, sem_s, sem_g1, sem_g2, sem_gs,
     sem_t, sem_y, sem_z, sem_v, sem_vy, sem_vz, sent,
-    tok, cnt, hid, gro, gain, rw, wg, wu, wd, sem_in,
+    tok, cnt, hid, gro, gain, rw, wg, wu, wd, wg_t, wu_t, sem_in,
 ):
     ny, nz, nx, width = sizes
     y, z, c, t, way = geometry(ny, nz, nx)
@@ -303,7 +303,7 @@
             same(G.at[zz, around(t + way, nx)], 8, sem_gs.at[i], x_to(-way)).wait_recv()
             same(G.at[zz, around(t + 2, nx)], 8, sem_g2.at[i], x_to(way)).wait_recv()
             g = G[zz].reshape(ny * rows, 3 * ff + AUX)
-            out = dot(g[:, 0:ff], wg[...], (1, 1)) + dot(g[:, ff:2 * ff], wu[...], (1, 1))
+            out = dot(g[:, 0:ff], wg_t[...], (1, 0)) + dot(g[:, ff:2 * ff], wu_t[...], (1, 0))
             part[zz, :, :, :, 0:cols] = out.astype(BF).reshape(ny, NC, CAP, cols)
             part[zz, :, :, :, cols:] = g[:, 3 * ff:].reshape(ny, NC, CAP, AUX)
             copy(part.at[zz, :, 1 - c], acc.at[zz], 9, sem_t.at[zz], partner).start()
@@ -382,6 +382,12 @@
         grad_up[columns] = both[:, ff:]
         grad_down[:, columns] = (dot(g[:, 2 * ff:], u, (0, 0)) * count_scale).astype(BF)
         return carry
+
+    def flip_gate():
+        wg_t[...] = wg[...].T
+
+    def flip_up():
+        wu_t[...] = wu[...].T
 
     tiles = cols // TILE
     last = nz - 1 + lag
@@ -405,11 +411,13 @@
         rows_backward(early(k, 5))
         y_start(early(k, 6))
         y_end(early(k, 7))
+        pl.when(k == 1)(flip_gate)
+        pl.when(k == 2)(flip_up)
         pl.when(k == last - 2)(sums_start)
         pl.when(k == last - 1)(sums_y)
         pl.when(k == last)(sums_z)
-        begin = jnp.clip((k - (last - 2)) * each, 0, tiles)
-        end = jnp.clip((k - (last - 3)) * each, 0, tiles)
+        begin = jnp.clip((k - (last - 2)) * 2, 0, tiles)
+        end = jnp.where(k == last, tiles, jnp.clip((k - (last - 3)) * 2, 0, tiles))
         lax.fori_loop(begin, end, tile, 0)
         return carry
 
@@ -504,7 +512,8 @@
             dma((nz,)), dma((nz, ny - 1)), dma((nz,)), dma((1,)), dma((ny,)), dma((nz,)), dma((15,)),
             scratch((1, CAP), jnp.int32), scratch((1, 1), jnp.int32),
             scratch(hidden_in.shape, BF), scratch(grad_out.shape, BF), scratch((1, cols), F32), scratch((1, cols), F32),
-            scratch((cols, ff), BF), scratch((cols, ff), BF), scratch((ff, cols), BF), dma((9,)),
+            scratch((cols, ff), BF), scratch((cols, ff), BF), scratch((ff, cols), BF),
+            scratch((ff, cols), BF), scratch((ff, cols), BF), dma((9,)),
         ],
         compiler_params=pltpu.CompilerParams(collective_id=0, has_side_effects=True, vmem_limit_bytes=60000000),
         name="block",

time: 114 us -> 112 us (0.982)
  Pallas kernels: 106 us -> 103 us
    pallas_call x1, Pallas kernels: 106 us -> 103 us  [body(): pl.pallas_call(functools.partial(kernel, sizes), out_shape=(scratch(grad_...]
where the time goes in v5:
time: 112 us; the launch traced here: 110 us
  Pallas kernels  103 us (92%)
  local copies, waits for them, and re-layouts  5.42 us (5%)
  between operations  1.29 us (1%)
    pallas_call x1, Pallas kernels, body(): pl.pallas_call(functools.partial(kernel, sizes), out_shape=(scratch(grad_...  103 us
    unnamed x6, local copies, waits for them, and re-layouts  5.42 us

profile of v5, /device:TPU:2, one launch (start us, length us, event | category | flops | bytes accessed | tf_op | source)
XLA Modules:
  0.0 109.7 jit_solution(11334082784772582601)
XLA Ops:
  1.3 103.0 %block.1 = (bf16[128,2048]{1,0:T(8,128)(2,1)S(1)}, bf16[2048,384]{1,0:T(8,128)(2,1)S(1)}, bf16[2048,384]{1,0:T(8,128)(2,1)S(1)}, bf16[384,2048]{1,0:T(8,128)(2,1...) custom-call(s32[1,16]{1,0:T(1,128)} %bitcast.11, s32[1,1]{1,0:T(1,128)} %bitcast.6.cnt_hbm, ...), custom_call_target="tpu_custom_call" | custom-call | tf_op jit(solution)/shard_map/block/pallas_call | solution.py:477
  104.3 0.8 copy.21
  105.1 0.6 copy.25
  105.7 0.6 copy.26
  106.3 1.1 %copy.22 = bf16[2048,384]{1,0:T(8,128)(2,1)} copy(bf16[2048,384]{1,0:T(8,128)(2,1)S(1)} %get-tuple-element.19) | data formatting | bytes 3145728
  107.4 1.1 %copy.23 = bf16[2048,384]{1,0:T(8,128)(2,1)} copy(bf16[2048,384]{1,0:T(8,128)(2,1)S(1)} %get-tuple-element.20) | data formatting | bytes 3145728
  108.6 1.1 %copy.24 = bf16[384,2048]{1,0:T(8,128)(2,1)} copy(bf16[384,2048]{1,0:T(8,128)(2,1)S(1)} %get-tuple-element.21) | data formatting | bytes 3145728
